TPU v7x, 32 devices: a whole 2x2x4 slice. The times are simulated.
32 devices in a mesh: data: 2 (over x), ctxo: 4 (over z), ctx: 4 (over y, core).
Axes of the slice: x: 2, y: 2, z: 4, core: 2. Of those that a mesh axis runs over, the one named last changes fastest.
Arguments:
- q_seq: bfloat16 [4, 6144, 7, 128], P('data', ('ctxo', 'ctx')), parts along dimension 0
- k_seq: bfloat16 [4, 6144, 1, 128], P('data', ('ctxo', 'ctx')), parts along dimension 0
- v_seq: bfloat16 [4, 6144, 1, 128], P('data', ('ctxo', 'ctx')), parts along dimension 0
- do_seq: bfloat16 [4, 6144, 7, 128], P('data', ('ctxo', 'ctx')), parts along dimension 0
Outputs:
- output 1: bfloat16 [4, 6144, 7, 128], P('data', ('ctxo', 'ctx')), parts along dimension 0
- output 2: bfloat16 [4, 6144, 7, 128], P('data', ('ctxo', 'ctx')), parts along dimension 0
- output 3: bfloat16 [4, 6144, 1, 128], P('data', ('ctxo', 'ctx')), parts along dimension 0
- output 4: bfloat16 [4, 6144, 1, 128], P('data', ('ctxo', 'ctx')), parts along dimension 0
There are 2 independent parts. A program takes and returns all parts, laid end to end along the dimension named above; each array names one.
All inputs are finite; a program needn't handle non-finite values.
Results may differ from a plain program's by a relative error of at most 0.0126409.
Values are sent between devices in bfloat16 or wider.
A program may use at most 1 GiB of HBM per device.

v0:
```python
import math
import jax
import jax.numpy as jnp
from jax import lax
from jax.sharding import PartitionSpec as P

CTX_AXES = ('ctxo', 'ctx')


def causal_mask(n_rows):
    row_ids = lax.broadcasted_iota(jnp.int32, (n_rows, 1, n_rows), 0)
    col_ids = lax.broadcasted_iota(jnp.int32, (n_rows, 1, n_rows), 2)
    return row_ids >= col_ids


def pair_forward(q_blk, k_blk, v_blk, key_mask):
    q_scale = 1.0 / math.sqrt(q_blk.shape[-1])
    scores = jnp.einsum('bqhgd,bkhd->bhqgk', q_blk, k_blk, preferred_element_type=jnp.float32) * q_scale
    if key_mask is not None:
        scores = jnp.where(key_mask, scores, -jnp.inf)
    row_max = jnp.max(scores, axis=-1)
    prob_blk = jnp.exp(scores - row_max[..., None])
    row_sum = jnp.sum(prob_blk, axis=-1)
    out_blk = jnp.einsum('bhqgk,bkhd->bhqgd', prob_blk.astype(jnp.bfloat16), v_blk, preferred_element_type=jnp.float32)
    return out_blk / row_sum[..., None], row_max + jnp.log(row_sum)


def merge_parts(out_a, lse_a, out_b, lse_b):
    lse_new = jnp.logaddexp(lse_a, lse_b)
    out_new = out_a * jnp.exp(lse_a - lse_new)[..., None] + out_b * jnp.exp(lse_b - lse_new)[..., None]
    return out_new, lse_new


def pair_backward(q_blk, do_blk, lse_blk, drow_blk, k_blk, v_blk, key_mask):
    q_scale = 1.0 / math.sqrt(q_blk.shape[-1])
    scores = jnp.einsum('bqhgd,bkhd->bhqgk', q_blk, k_blk, preferred_element_type=jnp.float32) * q_scale
    if key_mask is not None:
        scores = jnp.where(key_mask, scores, -jnp.inf)
    prob_blk = jnp.exp(scores - lse_blk[..., None])
    dv_part = jnp.einsum('bhqgk,bqhgd->bhkd', prob_blk.astype(jnp.bfloat16), do_blk, preferred_element_type=jnp.float32)
    prob_grad = jnp.einsum('bqhgd,bkhd->bhqgk', do_blk, v_blk, preferred_element_type=jnp.float32)
    score_grad = (prob_blk * (prob_grad - drow_blk[..., None])).astype(jnp.bfloat16)
    dq_part = jnp.einsum('bhqgk,bkhd->bhqgd', score_grad, k_blk, preferred_element_type=jnp.float32) * q_scale
    dk_part = jnp.einsum('bhqgk,bqhgd->bhkd', score_grad, q_blk, preferred_element_type=jnp.float32) * q_scale
    return dq_part, dk_part, dv_part


def solution(mesh):
    n_ctx = mesh.shape['ctxo'] * mesh.shape['ctx']
    half_ctx = n_ctx // 2
    next_perm = [(src_idx, (src_idx + 1) % n_ctx) for src_idx in range(n_ctx)]
    home_kv = [(src_idx, (src_idx - half_ctx) % n_ctx) for src_idx in range(n_ctx)]
    home_q = [(src_idx, (src_idx - half_ctx + 1) % n_ctx) for src_idx in range(n_ctx)]
    blk_spec = P('data', CTX_AXES, None, None)

    def send_next(tree_in):
        return lax.ppermute(tree_in, CTX_AXES, next_perm)

    def local_attn(q_in, k_in, v_in, do_in):
        batch_rows, chunk_len, q_heads, head_dim = q_in.shape
        kv_heads = k_in.shape[2]
        row_shape = (batch_rows, chunk_len, kv_heads, q_heads // kv_heads, head_dim)
        rank_idx = lax.axis_index(CTX_AXES)
        q_own = q_in.reshape(row_shape)
        do_own = do_in.reshape(row_shape)
        diag_mask = causal_mask(chunk_len)
        last_owner = rank_idx >= half_ctx

        own_out, own_lse = pair_forward(q_own, k_in, v_in, diag_mask)

        def fwd_step(step_idx, state_in):
            own_out, own_lse, k_buf, v_buf, q_buf, hlp_out, hlp_lse = state_in
            k_buf, v_buf, q_buf, hlp_out, hlp_lse = send_next((k_buf, v_buf, q_buf, hlp_out, hlp_lse))
            is_owner = rank_idx >= step_idx
            part_out, part_lse = pair_forward(jnp.where(is_owner, q_own, q_buf), jnp.where(is_owner, k_buf, k_in), jnp.where(is_owner, v_buf, v_in), None)
            new_out, new_lse = merge_parts(jnp.where(is_owner, own_out, hlp_out), jnp.where(is_owner, own_lse, hlp_lse), part_out, part_lse)
            own_out = jnp.where(is_owner, new_out, own_out)
            own_lse = jnp.where(is_owner, new_lse, own_lse)
            hlp_out = jnp.where(is_owner, hlp_out, new_out)
            hlp_lse = jnp.where(is_owner, hlp_lse, new_lse)
            return own_out, own_lse, k_buf, v_buf, q_buf, hlp_out, hlp_lse

        fwd_state = (own_out, own_lse, k_in, v_in, q_own, jnp.zeros_like(own_out), jnp.full_like(own_lse, -jnp.inf))
        own_out, own_lse, k_buf, v_buf, q_buf, hlp_out, hlp_lse = lax.fori_loop(1, half_ctx, fwd_step, fwd_state)
        k_buf, v_buf = send_next((k_buf, v_buf))
        part_out, part_lse = pair_forward(q_own, k_buf, v_buf, None)
        new_out, new_lse = merge_parts(own_out, own_lse, part_out, part_lse)
        own_out = jnp.where(last_owner, new_out, own_out)
        own_lse = jnp.where(last_owner, new_lse, own_lse)
        hlp_out, hlp_lse = lax.ppermute((hlp_out, hlp_lse), CTX_AXES, home_q)
        own_out, own_lse = merge_parts(own_out, own_lse, hlp_out, hlp_lse)

        drow_own = jnp.sum(jnp.swapaxes(do_own, 1, 2) * own_out, axis=-1)
        dq_own, dk_own, dv_own = pair_backward(q_own, do_own, own_lse, drow_own, k_in, v_in, diag_mask)

        def bwd_step(step_idx, state_in):
            dq_own, dk_own, dv_own, kv_bundle, q_bundle = state_in
            kv_bundle, q_bundle = send_next((kv_bundle, q_bundle))
            k_buf, v_buf, dk_buf, dv_buf = kv_bundle
            q_buf, do_buf, lse_buf, drow_buf, dq_buf = q_bundle
            is_owner = rank_idx >= step_idx
            dq_part, dk_part, dv_part = pair_backward(
                jnp.where(is_owner, q_own, q_buf), jnp.where(is_owner, do_own, do_buf),
                jnp.where(is_owner, own_lse, lse_buf), jnp.where(is_owner, drow_own, drow_buf),
                jnp.where(is_owner, k_buf, k_in), jnp.where(is_owner, v_buf, v_in), None)
            dq_own = jnp.where(is_owner, dq_own + dq_part, dq_own)
            dk_own = jnp.where(is_owner, dk_own, dk_own + dk_part)
            dv_own = jnp.where(is_owner, dv_own, dv_own + dv_part)
            kv_bundle = (k_buf, v_buf, jnp.where(is_owner, dk_buf + dk_part, dk_buf), jnp.where(is_owner, dv_buf + dv_part, dv_buf))
            q_bundle = (q_buf, do_buf, lse_buf, drow_buf, jnp.where(is_owner, dq_buf, dq_buf + dq_part))
            return dq_own, dk_own, dv_own, kv_bundle, q_bundle

        kv_bundle = (k_in, v_in, jnp.zeros_like(dk_own), jnp.zeros_like(dv_own))
        q_bundle = (q_own, do_own, own_lse, drow_own, jnp.zeros_like(dq_own))
        dq_own, dk_own, dv_own, kv_bundle, q_bundle = lax.fori_loop(1, half_ctx, bwd_step, (dq_own, dk_own, dv_own, kv_bundle, q_bundle))
        k_buf, v_buf, dk_buf, dv_buf = send_next(kv_bundle)
        dq_part, dk_part, dv_part = pair_backward(q_own, do_own, own_lse, drow_own, k_buf, v_buf, None)
        dq_own = jnp.where(last_owner, dq_own + dq_part, dq_own)
        dk_buf = jnp.where(last_owner, dk_buf + dk_part, dk_buf)
        dv_buf = jnp.where(last_owner, dv_buf + dv_part, dv_buf)
        dk_buf, dv_buf = lax.ppermute((dk_buf, dv_buf), CTX_AXES, home_kv)
        dq_buf = lax.ppermute(q_bundle[4], CTX_AXES, home_q)
        out_seq = jnp.swapaxes(own_out.astype(jnp.bfloat16), 1, 2).reshape(q_in.shape)
        dq_seq = jnp.swapaxes((dq_own + dq_buf).astype(jnp.bfloat16), 1, 2).reshape(q_in.shape)
        dk_seq = jnp.swapaxes((dk_own + dk_buf).astype(jnp.bfloat16), 1, 2)
        dv_seq = jnp.swapaxes((dv_own + dv_buf).astype(jnp.bfloat16), 1, 2)
        return out_seq, dq_seq, dk_seq, dv_seq

    return jax.shard_map(local_attn, mesh=mesh, in_specs=(blk_spec, blk_spec, blk_spec, blk_spec), out_specs=(blk_spec, blk_spec, blk_spec, blk_spec), check_vma=False)
```

profile of v0, /device:TPU:27, one launch (start us, length us, event | category | flops | bytes accessed | tf_op | source)
XLA Modules:
  0.0 1476.0 jit_solution(18088287411203895945)
XLA Ops:
  13.0 466.8 %while.62 = (s32[]{:T(128)}, f32[2,1,384,7,128]{4,2,3,0,1:T(8,128)}, f32[2,1,384,7]{2,3,0,1:T(8,128)}, bf16[2,384,1,128]{3,1,0,2:T(8,128)(2,1)}, bf16[2,384,1,12...) while((s32[]{:T(128)}, ...), condition=%wide.region_5.6_spmd.clone, body=%wide.region_2.5_spmd.clone.sunk | while | flops 1079950080 | bytes 89312752 | solution.py:84
  19.1 42.6 %collective-permute-done.2 = bf16[2,384,1,128]{3,1,0,2:T(8,128)(2,1)S(1)} collective-permute-done((bf16[2,384,1,128]{3,1,0,2:T(8,128)(2,1)}, bf16[2,384,1,128]{3,1,0,2:T(8,128)(2,1)S(1)}, u32[]{:S(2)}, u32[]{:S(2)}) %collective-permute-start.2) | collective-permute-done | bytes 196640 | tf_op jit(solution)/shard_map/while/body/eval_jaxpr/ppermute | solution.py:57
  69.9 7.2 broadcast_select_fusion.31
  89.0 39.0 %collective-permute-done.2 = bf16[2,384,1,128]{3,1,0,2:T(8,128)(2,1)S(1)} collective-permute-done((bf16[2,384,1,128]{3,1,0,2:T(8,128)(2,1)}, bf16[2,384,1,128]{3,1,0,2:T(8,128)(2,1)S(1)}, u32[]{:S(2)}, u32[]{:S(2)}) %collective-permute-start.2) | collective-permute-done | bytes 196640 | tf_op jit(solution)/shard_map/while/body/eval_jaxpr/ppermute | solution.py:57
  136.1 7.2 broadcast_select_fusion.31
  152.1 5.9 collective-permute-start.2
  158.7 35.5 %collective-permute-done.2 = bf16[2,384,1,128]{3,1,0,2:T(8,128)(2,1)S(1)} collective-permute-done((bf16[2,384,1,128]{3,1,0,2:T(8,128)(2,1)}, bf16[2,384,1,128]{3,1,0,2:T(8,128)(2,1)S(1)}, u32[]{:S(2)}, u32[]{:S(2)}) %collective-permute-start.2) | collective-permute-done | bytes 196640 | tf_op jit(solution)/shard_map/while/body/eval_jaxpr/ppermute | solution.py:57
  202.4 7.2 broadcast_select_fusion.31
  221.8 5.9 collective-permute-start.2
  228.3 32.1 %collective-permute-done.2 = bf16[2,384,1,128]{3,1,0,2:T(8,128)(2,1)S(1)} collective-permute-done((bf16[2,384,1,128]{3,1,0,2:T(8,128)(2,1)}, bf16[2,384,1,128]{3,1,0,2:T(8,128)(2,1)S(1)}, u32[]{:S(2)}, u32[]{:S(2)}) %collective-permute-start.2) | collective-permute-done | bytes 196640 | tf_op jit(solution)/shard_map/while/body/eval_jaxpr/ppermute | solution.py:57
  268.7 7.2 broadcast_select_fusion.31
  283.4 8.0 collective-permute-start
  291.5 5.9 collective-permute-start.2
  298.0 28.7 %collective-permute-done.2 = bf16[2,384,1,128]{3,1,0,2:T(8,128)(2,1)S(1)} collective-permute-done((bf16[2,384,1,128]{3,1,0,2:T(8,128)(2,1)}, bf16[2,384,1,128]{3,1,0,2:T(8,128)(2,1)S(1)}, u32[]{:S(2)}, u32[]{:S(2)}) %collective-permute-start.2) | collective-permute-done | bytes 196640 | tf_op jit(solution)/shard_map/while/body/eval_jaxpr/ppermute | solution.py:57
  334.9 7.2 broadcast_select_fusion.31
  349.7 11.5 collective-permute-start
  361.1 5.9 collective-permute-start.2
  367.7 25.5 %collective-permute-done.2 = bf16[2,384,1,128]{3,1,0,2:T(8,128)(2,1)S(1)} collective-permute-done((bf16[2,384,1,128]{3,1,0,2:T(8,128)(2,1)}, bf16[2,384,1,128]{3,1,0,2:T(8,128)(2,1)S(1)}, u32[]{:S(2)}, u32[]{:S(2)}) %collective-permute-start.2) | collective-permute-done | bytes 196640 | tf_op jit(solution)/shard_map/while/body/eval_jaxpr/ppermute | solution.py:57
  401.4 7.2 broadcast_select_fusion.31
  416.2 14.6 collective-permute-start
  430.8 5.9 collective-permute-start.2
  437.4 25.5 %collective-permute-done.2 = bf16[2,384,1,128]{3,1,0,2:T(8,128)(2,1)S(1)} collective-permute-done((bf16[2,384,1,128]{3,1,0,2:T(8,128)(2,1)}, bf16[2,384,1,128]{3,1,0,2:T(8,128)(2,1)S(1)}, u32[]{:S(2)}, u32[]{:S(2)}) %collective-permute-start.2) | collective-permute-done | bytes 196640 | tf_op jit(solution)/shard_map/while/body/eval_jaxpr/ppermute | solution.py:57
  471.1 7.2 broadcast_select_fusion.31
  486.5 19.8 %collective-permute-start.16 = (f32[2,1,384,7]{2,3,0,1:T(8,128)S(1)}, f32[2,1,384,7]{2,3,0,1:T(8,128)}, u32[]{:S(2)}, u32[]{:S(2)}) collective-permute-start(f32[2,1,384,7]{2,3,0,1:T(8,128)S(1)} %copy-done.25), channel_id=1, source_target_pairs={{0,9},{1,10},{2,11},{3,12},{4,13},{5,14},{6,15},{7,0},{8,1},{9,2},... | collective-permute-start | bytes 64520 | tf_op jit(solution)/shard_map/ppermute | solution.py:90
  519.8 84.1 %collective-permute-done.16 = f32[2,1,384,7]{2,3,0,1:T(8,128)} collective-permute-done((f32[2,1,384,7]{2,3,0,1:T(8,128)S(1)}, f32[2,1,384,7]{2,3,0,1:T(8,128)}, u32[]{:S(2)}, u32[]{:S(2)}) %collective-permute-start.16) | collective-permute-done | bytes 21536 | tf_op jit(solution)/shard_map/ppermute | solution.py:90
  606.7 6.1 fusion.89
  613.7 6.6 fusion.84
  632.4 669.9 %while.63 = (s32[]{:T(128)}, f32[2,1,384,7,128]{4,2,3,0,1:T(8,128)}, f32[2,1,384,128]{3,2,0,1:T(8,128)S(1)}, f32[2,1,384,128]{3,2,0,1:T(8,128)}, bf16[2,384,1,12...) while((s32[]{:T(128)}, ...), condition=%wide.region_10.11_spmd.clone, body=%wide.region_9.10_spmd.clone.sunk | while | flops 2667194880 | bytes 137094928 | solution.py:115
  642.1 24.6 %collective-permute-done.9 = f32[2,1,384,7]{2,3,0,1:T(8,128)} collective-permute-done((f32[2,1,384,7]{2,3,0,1:T(8,128)}, f32[2,1,384,7]{2,3,0,1:T(8,128)}, u32[]{:S(2)}, u32[]{:S(2)}) %collective-permute-start.9) | collective-permute-done | bytes 21536 | tf_op jit(solution)/shard_map/while/body/eval_jaxpr/ppermute | solution.py:57
  674.2 27.1 %collective-permute-done.11 = bf16[2,384,1,128]{3,1,0,2:T(8,128)(2,1)S(1)} collective-permute-done((bf16[2,384,1,128]{3,1,0,2:T(8,128)(2,1)}, bf16[2,384,1,128]{3,1,0,2:T(8,128)(2,1)S(1)}, u32[]{:S(2)}, u32[]{:S(2)}) %collective-permute-start.11) | collective-permute-done | bytes 196640 | tf_op jit(solution)/shard_map/while/body/eval_jaxpr/ppermute | solution.py:57
  736.9 21.8 %collective-permute-done.9 = f32[2,1,384,7]{2,3,0,1:T(8,128)} collective-permute-done((f32[2,1,384,7]{2,3,0,1:T(8,128)}, f32[2,1,384,7]{2,3,0,1:T(8,128)}, u32[]{:S(2)}, u32[]{:S(2)}) %collective-permute-start.9) | collective-permute-done | bytes 21536 | tf_op jit(solution)/shard_map/while/body/eval_jaxpr/ppermute | solution.py:57
  770.8 22.5 %collective-permute-done.11 = bf16[2,384,1,128]{3,1,0,2:T(8,128)(2,1)S(1)} collective-permute-done((bf16[2,384,1,128]{3,1,0,2:T(8,128)(2,1)}, bf16[2,384,1,128]{3,1,0,2:T(8,128)(2,1)S(1)}, u32[]{:S(2)}, u32[]{:S(2)}) %collective-permute-start.11) | collective-permute-done | bytes 196640 | tf_op jit(solution)/shard_map/while/body/eval_jaxpr/ppermute | solution.py:57
  832.0 20.9 %collective-permute-done.9 = f32[2,1,384,7]{2,3,0,1:T(8,128)} collective-permute-done((f32[2,1,384,7]{2,3,0,1:T(8,128)}, f32[2,1,384,7]{2,3,0,1:T(8,128)}, u32[]{:S(2)}, u32[]{:S(2)}) %collective-permute-start.9) | collective-permute-done | bytes 21536 | tf_op jit(solution)/shard_map/while/body/eval_jaxpr/ppermute | solution.py:57
  868.2 19.3 %collective-permute-done.11 = bf16[2,384,1,128]{3,1,0,2:T(8,128)(2,1)S(1)} collective-permute-done((bf16[2,384,1,128]{3,1,0,2:T(8,128)(2,1)}, bf16[2,384,1,128]{3,1,0,2:T(8,128)(2,1)S(1)}, u32[]{:S(2)}, u32[]{:S(2)}) %collective-permute-start.11) | collective-permute-done | bytes 196640 | tf_op jit(solution)/shard_map/while/body/eval_jaxpr/ppermute | solution.py:57
  912.6 5.4 collective-permute-start.6
  929.4 20.9 %collective-permute-done.9 = f32[2,1,384,7]{2,3,0,1:T(8,128)} collective-permute-done((f32[2,1,384,7]{2,3,0,1:T(8,128)}, f32[2,1,384,7]{2,3,0,1:T(8,128)}, u32[]{:S(2)}, u32[]{:S(2)}) %collective-permute-start.9) | collective-permute-done | bytes 21536 | tf_op jit(solution)/shard_map/while/body/eval_jaxpr/ppermute | solution.py:57
  965.7 19.3 %collective-permute-done.11 = bf16[2,384,1,128]{3,1,0,2:T(8,128)(2,1)S(1)} collective-permute-done((bf16[2,384,1,128]{3,1,0,2:T(8,128)(2,1)}, bf16[2,384,1,128]{3,1,0,2:T(8,128)(2,1)S(1)}, u32[]{:S(2)}, u32[]{:S(2)}) %collective-permute-start.11) | collective-permute-done | bytes 196640 | tf_op jit(solution)/shard_map/while/body/eval_jaxpr/ppermute | solution.py:57
  1010.0 5.4 collective-permute-start.6
  1026.9 20.9 %collective-permute-done.9 = f32[2,1,384,7]{2,3,0,1:T(8,128)} collective-permute-done((f32[2,1,384,7]{2,3,0,1:T(8,128)}, f32[2,1,384,7]{2,3,0,1:T(8,128)}, u32[]{:S(2)}, u32[]{:S(2)}) %collective-permute-start.9) | collective-permute-done | bytes 21536 | tf_op jit(solution)/shard_map/while/body/eval_jaxpr/ppermute | solution.py:57
  1063.1 19.3 %collective-permute-done.11 = bf16[2,384,1,128]{3,1,0,2:T(8,128)(2,1)S(1)} collective-permute-done((bf16[2,384,1,128]{3,1,0,2:T(8,128)(2,1)}, bf16[2,384,1,128]{3,1,0,2:T(8,128)(2,1)S(1)}, u32[]{:S(2)}, u32[]{:S(2)}) %collective-permute-start.11) | collective-permute-done | bytes 196640 | tf_op jit(solution)/shard_map/while/body/eval_jaxpr/ppermute | solution.py:57
  1107.4 5.4 collective-permute-start.6
  1124.3 20.9 %collective-permute-done.9 = f32[2,1,384,7]{2,3,0,1:T(8,128)} collective-permute-done((f32[2,1,384,7]{2,3,0,1:T(8,128)}, f32[2,1,384,7]{2,3,0,1:T(8,128)}, u32[]{:S(2)}, u32[]{:S(2)}) %collective-permute-start.9) | collective-permute-done | bytes 21536 | tf_op jit(solution)/shard_map/while/body/eval_jaxpr/ppermute | solution.py:57
  1160.5 19.3 %collective-permute-done.11 = bf16[2,384,1,128]{3,1,0,2:T(8,128)(2,1)S(1)} collective-permute-done((bf16[2,384,1,128]{3,1,0,2:T(8,128)(2,1)}, bf16[2,384,1,128]{3,1,0,2:T(8,128)(2,1)S(1)}, u32[]{:S(2)}, u32[]{:S(2)}) %collective-permute-start.11) | collective-permute-done | bytes 196640 | tf_op jit(solution)/shard_map/while/body/eval_jaxpr/ppermute | solution.py:57
  1204.9 5.4 collective-permute-start.6
  1221.7 20.9 %collective-permute-done.9 = f32[2,1,384,7]{2,3,0,1:T(8,128)} collective-permute-done((f32[2,1,384,7]{2,3,0,1:T(8,128)}, f32[2,1,384,7]{2,3,0,1:T(8,128)}, u32[]{:S(2)}, u32[]{:S(2)}) %collective-permute-start.9) | collective-permute-done | bytes 21536 | tf_op jit(solution)/shard_map/while/body/eval_jaxpr/ppermute | solution.py:57
  1258.0 19.3 %collective-permute-done.11 = bf16[2,384,1,128]{3,1,0,2:T(8,128)(2,1)S(1)} collective-permute-done((bf16[2,384,1,128]{3,1,0,2:T(8,128)(2,1)}, bf16[2,384,1,128]{3,1,0,2:T(8,128)(2,1)S(1)}, u32[]{:S(2)}, u32[]{:S(2)}) %collective-permute-start.11) | collective-permute-done | bytes 196640 | tf_op jit(solution)/shard_map/while/body/eval_jaxpr/ppermute | solution.py:57
  1336.6 123.4 %collective-permute-done.24 = f32[2,1,384,128]{3,2,0,1:T(8,128)} collective-permute-done((f32[2,1,384,128]{3,2,0,1:T(8,128)}, f32[2,1,384,128]{3,2,0,1:T(8,128)}, u32[]{:S(2)}, u32[]{:S(2)}) %collective-permute-start.24) | collective-permute-done | bytes 393248 | tf_op jit(solution)/shard_map/ppermute | solution.py:121
  1461.8 6.6 collective-permute-done.22
  (600 shorter events, 565.5 us)
Async XLA Ops:
  13.0 51.4 %collective-permute-start.3 = (bf16[2,384,1,7,128]{4,1,3,0,2:T(8,128)(2,1)}, bf16[2,384,1,7,128]{4,1,3,0,2:T(8,128)(2,1)S(1)}, u32[]{:S(2)}, u32[]{:S(2)}) collective-permute-start(bf16[2,384,1,7,128]{4,1,3,0,2:T(8,128)(2,1)} %get-tuple-element.1019), channel_id=1, source_target_pairs={{0,1},{1,2},{2,3},{3,4},{4,5},{5,6},{6,7},{7,8},{8,9},{9,10},{10,1... | collective-permute-start | bytes 4128776 | tf_op jit(solution)/shard_map/while/body/eval_jaxpr/ppermute | solution.py:57
  16.6 53.3 %collective-permute-start = (f32[2,1,384,7,128]{4,2,3,0,1:T(8,128)}, f32[2,1,384,7,128]{4,2,3,0,1:T(8,128)}, u32[]{:S(2)}, u32[]{:S(2)}) collective-permute-start(f32[2,1,384,7,128]{4,2,3,0,1:T(8,128)} %broadcast_select_fusion.27), channel_id=1, source_target_pairs={{0,1},{1,2},{2,3},{3,4},{4,5},{5,6},{6,7},{7,8},{8,9},{9,10},{10,1... | collective-permute-start | bytes 8257544 | tf_op jit(solution)/shard_map/while/body/eval_jaxpr/ppermute | solution.py:57
  16.6 45.1 %collective-permute-start.2 = (bf16[2,384,1,128]{3,1,0,2:T(8,128)(2,1)}, bf16[2,384,1,128]{3,1,0,2:T(8,128)(2,1)S(1)}, u32[]{:S(2)}, u32[]{:S(2)}) collective-permute-start(bf16[2,384,1,128]{3,1,0,2:T(8,128)(2,1)} %get-tuple-element.1017), channel_id=1, source_target_pairs={{0,1},{1,2},{2,3},{3,4},{4,5},{5,6},{6,7},{7,8},{8,9},{9,10},{10,1... | collective-permute-start | bytes 589832 | tf_op jit(solution)/shard_map/while/body/eval_jaxpr/ppermute | solution.py:57
  16.9 46.9 %collective-permute-start.4 = (bf16[2,384,1,128]{3,1,0,2:T(8,128)(2,1)}, bf16[2,384,1,128]{3,1,0,2:T(8,128)(2,1)S(1)}, u32[]{:S(2)}, u32[]{:S(2)}) collective-permute-start(bf16[2,384,1,128]{3,1,0,2:T(8,128)(2,1)} %get-tuple-element.1018), channel_id=1, source_target_pairs={{0,1},{1,2},{2,3},{3,4},{4,5},{5,6},{6,7},{7,8},{8,9},{9,10},{10,1... | collective-permute-start | bytes 589832 | tf_op jit(solution)/shard_map/while/body/eval_jaxpr/ppermute | solution.py:57
  17.5 50.7 %collective-permute-start.1 = (f32[2,1,384,7]{2,3,0,1:T(8,128)}, f32[2,1,384,7]{2,3,0,1:T(8,128)}, u32[]{:S(2)}, u32[]{:S(2)}) collective-permute-start(f32[2,1,384,7]{2,3,0,1:T(8,128)} %broadcast_select_fusion.28), channel_id=1, source_target_pairs={{0,1},{1,2},{2,3},{3,4},{4,5},{5,6},{6,7},{7,8},{8,9},{9,10},{10,1... | collective-permute-start | bytes 64520 | tf_op jit(solution)/shard_map/while/body/eval_jaxpr/ppermute | solution.py:57
  78.6 52.1 %collective-permute-start.3 = (bf16[2,384,1,7,128]{4,1,3,0,2:T(8,128)(2,1)}, bf16[2,384,1,7,128]{4,1,3,0,2:T(8,128)(2,1)S(1)}, u32[]{:S(2)}, u32[]{:S(2)}) collective-permute-start(bf16[2,384,1,7,128]{4,1,3,0,2:T(8,128)(2,1)} %get-tuple-element.1019), channel_id=1, source_target_pairs={{0,1},{1,2},{2,3},{3,4},{4,5},{5,6},{6,7},{7,8},{8,9},{9,10},{10,1... | collective-permute-start | bytes 4128776 | tf_op jit(solution)/shard_map/while/body/eval_jaxpr/ppermute | solution.py:57
  84.6 51.5 %collective-permute-start = (f32[2,1,384,7,128]{4,2,3,0,1:T(8,128)}, f32[2,1,384,7,128]{4,2,3,0,1:T(8,128)}, u32[]{:S(2)}, u32[]{:S(2)}) collective-permute-start(f32[2,1,384,7,128]{4,2,3,0,1:T(8,128)} %broadcast_select_fusion.27), channel_id=1, source_target_pairs={{0,1},{1,2},{2,3},{3,4},{4,5},{5,6},{6,7},{7,8},{8,9},{9,10},{10,1... | collective-permute-start | bytes 8257544 | tf_op jit(solution)/shard_map/while/body/eval_jaxpr/ppermute | solution.py:57
  84.6 43.3 %collective-permute-start.2 = (bf16[2,384,1,128]{3,1,0,2:T(8,128)(2,1)}, bf16[2,384,1,128]{3,1,0,2:T(8,128)(2,1)S(1)}, u32[]{:S(2)}, u32[]{:S(2)}) collective-permute-start(bf16[2,384,1,128]{3,1,0,2:T(8,128)(2,1)} %get-tuple-element.1017), channel_id=1, source_target_pairs={{0,1},{1,2},{2,3},{3,4},{4,5},{5,6},{6,7},{7,8},{8,9},{9,10},{10,1... | collective-permute-start | bytes 589832 | tf_op jit(solution)/shard_map/while/body/eval_jaxpr/ppermute | solution.py:57
  89.0 45.5 %collective-permute-start.1 = (f32[2,1,384,7]{2,3,0,1:T(8,128)}, f32[2,1,384,7]{2,3,0,1:T(8,128)}, u32[]{:S(2)}, u32[]{:S(2)}) collective-permute-start(f32[2,1,384,7]{2,3,0,1:T(8,128)} %broadcast_select_fusion.28), channel_id=1, source_target_pairs={{0,1},{1,2},{2,3},{3,4},{4,5},{5,6},{6,7},{7,8},{8,9},{9,10},{10,1... | collective-permute-start | bytes 64520 | tf_op jit(solution)/shard_map/while/body/eval_jaxpr/ppermute | solution.py:57
  144.9 52.1 %collective-permute-start.3 = (bf16[2,384,1,7,128]{4,1,3,0,2:T(8,128)(2,1)}, bf16[2,384,1,7,128]{4,1,3,0,2:T(8,128)(2,1)S(1)}, u32[]{:S(2)}, u32[]{:S(2)}) collective-permute-start(bf16[2,384,1,7,128]{4,1,3,0,2:T(8,128)(2,1)} %get-tuple-element.1019), channel_id=1, source_target_pairs={{0,1},{1,2},{2,3},{3,4},{4,5},{5,6},{6,7},{7,8},{8,9},{9,10},{10,1... | collective-permute-start | bytes 4128776 | tf_op jit(solution)/shard_map/while/body/eval_jaxpr/ppermute | solution.py:57
  150.9 51.5 %collective-permute-start = (f32[2,1,384,7,128]{4,2,3,0,1:T(8,128)}, f32[2,1,384,7,128]{4,2,3,0,1:T(8,128)}, u32[]{:S(2)}, u32[]{:S(2)}) collective-permute-start(f32[2,1,384,7,128]{4,2,3,0,1:T(8,128)} %broadcast_select_fusion.27), channel_id=1, source_target_pairs={{0,1},{1,2},{2,3},{3,4},{4,5},{5,6},{6,7},{7,8},{8,9},{9,10},{10,1... | collective-permute-start | bytes 8257544 | tf_op jit(solution)/shard_map/while/body/eval_jaxpr/ppermute | solution.py:57
  152.1 42.1 %collective-permute-start.2 = (bf16[2,384,1,128]{3,1,0,2:T(8,128)(2,1)}, bf16[2,384,1,128]{3,1,0,2:T(8,128)(2,1)S(1)}, u32[]{:S(2)}, u32[]{:S(2)}) collective-permute-start(bf16[2,384,1,128]{3,1,0,2:T(8,128)(2,1)} %get-tuple-element.1017), channel_id=1, source_target_pairs={{0,1},{1,2},{2,3},{3,4},{4,5},{5,6},{6,7},{7,8},{8,9},{9,10},{10,1... | collective-permute-start | bytes 589832 | tf_op jit(solution)/shard_map/while/body/eval_jaxpr/ppermute | solution.py:57
  158.7 42.1 %collective-permute-start.1 = (f32[2,1,384,7]{2,3,0,1:T(8,128)}, f32[2,1,384,7]{2,3,0,1:T(8,128)}, u32[]{:S(2)}, u32[]{:S(2)}) collective-permute-start(f32[2,1,384,7]{2,3,0,1:T(8,128)} %broadcast_select_fusion.28), channel_id=1, source_target_pairs={{0,1},{1,2},{2,3},{3,4},{4,5},{5,6},{6,7},{7,8},{8,9},{9,10},{10,1... | collective-permute-start | bytes 64520 | tf_op jit(solution)/shard_map/while/body/eval_jaxpr/ppermute | solution.py:57
  211.1 52.1 %collective-permute-start.3 = (bf16[2,384,1,7,128]{4,1,3,0,2:T(8,128)(2,1)}, bf16[2,384,1,7,128]{4,1,3,0,2:T(8,128)(2,1)S(1)}, u32[]{:S(2)}, u32[]{:S(2)}) collective-permute-start(bf16[2,384,1,7,128]{4,1,3,0,2:T(8,128)(2,1)} %get-tuple-element.1019), channel_id=1, source_target_pairs={{0,1},{1,2},{2,3},{3,4},{4,5},{5,6},{6,7},{7,8},{8,9},{9,10},{10,1... | collective-permute-start | bytes 4128776 | tf_op jit(solution)/shard_map/while/body/eval_jaxpr/ppermute | solution.py:57
  217.2 51.5 %collective-permute-start = (f32[2,1,384,7,128]{4,2,3,0,1:T(8,128)}, f32[2,1,384,7,128]{4,2,3,0,1:T(8,128)}, u32[]{:S(2)}, u32[]{:S(2)}) collective-permute-start(f32[2,1,384,7,128]{4,2,3,0,1:T(8,128)} %broadcast_select_fusion.27), channel_id=1, source_target_pairs={{0,1},{1,2},{2,3},{3,4},{4,5},{5,6},{6,7},{7,8},{8,9},{9,10},{10,1... | collective-permute-start | bytes 8257544 | tf_op jit(solution)/shard_map/while/body/eval_jaxpr/ppermute | solution.py:57
  277.4 52.1 %collective-permute-start.3 = (bf16[2,384,1,7,128]{4,1,3,0,2:T(8,128)(2,1)}, bf16[2,384,1,7,128]{4,1,3,0,2:T(8,128)(2,1)S(1)}, u32[]{:S(2)}, u32[]{:S(2)}) collective-permute-start(bf16[2,384,1,7,128]{4,1,3,0,2:T(8,128)(2,1)} %get-tuple-element.1019), channel_id=1, source_target_pairs={{0,1},{1,2},{2,3},{3,4},{4,5},{5,6},{6,7},{7,8},{8,9},{9,10},{10,1... | collective-permute-start | bytes 4128776 | tf_op jit(solution)/shard_map/while/body/eval_jaxpr/ppermute | solution.py:57
  283.4 51.5 %collective-permute-start = (f32[2,1,384,7,128]{4,2,3,0,1:T(8,128)}, f32[2,1,384,7,128]{4,2,3,0,1:T(8,128)}, u32[]{:S(2)}, u32[]{:S(2)}) collective-permute-start(f32[2,1,384,7,128]{4,2,3,0,1:T(8,128)} %broadcast_select_fusion.27), channel_id=1, source_target_pairs={{0,1},{1,2},{2,3},{3,4},{4,5},{5,6},{6,7},{7,8},{8,9},{9,10},{10,1... | collective-permute-start | bytes 8257544 | tf_op jit(solution)/shard_map/while/body/eval_jaxpr/ppermute | solution.py:57
  343.7 52.4 %collective-permute-start.3 = (bf16[2,384,1,7,128]{4,1,3,0,2:T(8,128)(2,1)}, bf16[2,384,1,7,128]{4,1,3,0,2:T(8,128)(2,1)S(1)}, u32[]{:S(2)}, u32[]{:S(2)}) collective-permute-start(bf16[2,384,1,7,128]{4,1,3,0,2:T(8,128)(2,1)} %get-tuple-element.1019), channel_id=1, source_target_pairs={{0,1},{1,2},{2,3},{3,4},{4,5},{5,6},{6,7},{7,8},{8,9},{9,10},{10,1... | collective-permute-start | bytes 4128776 | tf_op jit(solution)/shard_map/while/body/eval_jaxpr/ppermute | solution.py:57
  349.7 51.7 %collective-permute-start = (f32[2,1,384,7,128]{4,2,3,0,1:T(8,128)}, f32[2,1,384,7,128]{4,2,3,0,1:T(8,128)}, u32[]{:S(2)}, u32[]{:S(2)}) collective-permute-start(f32[2,1,384,7,128]{4,2,3,0,1:T(8,128)} %broadcast_select_fusion.27), channel_id=1, source_target_pairs={{0,1},{1,2},{2,3},{3,4},{4,5},{5,6},{6,7},{7,8},{8,9},{9,10},{10,1... | collective-permute-start | bytes 8257544 | tf_op jit(solution)/shard_map/while/body/eval_jaxpr/ppermute | solution.py:57
  410.2 55.5 %collective-permute-start.3 = (bf16[2,384,1,7,128]{4,1,3,0,2:T(8,128)(2,1)}, bf16[2,384,1,7,128]{4,1,3,0,2:T(8,128)(2,1)S(1)}, u32[]{:S(2)}, u32[]{:S(2)}) collective-permute-start(bf16[2,384,1,7,128]{4,1,3,0,2:T(8,128)(2,1)} %get-tuple-element.1019), channel_id=1, source_target_pairs={{0,1},{1,2},{2,3},{3,4},{4,5},{5,6},{6,7},{7,8},{8,9},{9,10},{10,1... | collective-permute-start | bytes 4128776 | tf_op jit(solution)/shard_map/while/body/eval_jaxpr/ppermute | solution.py:57
  416.2 54.9 %collective-permute-start = (f32[2,1,384,7,128]{4,2,3,0,1:T(8,128)}, f32[2,1,384,7,128]{4,2,3,0,1:T(8,128)}, u32[]{:S(2)}, u32[]{:S(2)}) collective-permute-start(f32[2,1,384,7,128]{4,2,3,0,1:T(8,128)} %broadcast_select_fusion.27), channel_id=1, source_target_pairs={{0,1},{1,2},{2,3},{3,4},{4,5},{5,6},{6,7},{7,8},{8,9},{9,10},{10,1... | collective-permute-start | bytes 8257544 | tf_op jit(solution)/shard_map/while/body/eval_jaxpr/ppermute | solution.py:57
  483.2 130.5 %collective-permute-start.17 = (f32[2,1,384,7,128]{2,4,3,0,1:T(8,128)}, f32[2,1,384,7,128]{2,4,3,0,1:T(8,128)}, u32[]{:S(2)}, u32[]{:S(2)}) collective-permute-start(f32[2,1,384,7,128]{2,4,3,0,1:T(8,128)} %copy.20), channel_id=1, source_target_pairs={{0,9},{1,10},{2,11},{3,12},{4,13},{5,14},{6,15},{7,0},{8,1},{9,2},... | collective-permute-start | bytes 8257544 | tf_op jit(solution)/shard_map/ppermute | solution.py:90
  486.5 117.5 %collective-permute-start.16 = (f32[2,1,384,7]{2,3,0,1:T(8,128)S(1)}, f32[2,1,384,7]{2,3,0,1:T(8,128)}, u32[]{:S(2)}, u32[]{:S(2)}) collective-permute-start(f32[2,1,384,7]{2,3,0,1:T(8,128)S(1)} %copy-done.25), channel_id=1, source_target_pairs={{0,9},{1,10},{2,11},{3,12},{4,13},{5,14},{6,15},{7,0},{8,1},{9,2},... | collective-permute-start | bytes 64520 | tf_op jit(solution)/shard_map/ppermute | solution.py:90
  507.3 106.3 %collective-permute-start.15 = (bf16[2,384,1,128]{1,3,0,2:T(8,128)(2,1)S(1)}, bf16[2,384,1,128]{1,3,0,2:T(8,128)(2,1)}, u32[]{:S(2)}, u32[]{:S(2)}) collective-permute-start(bf16[2,384,1,128]{1,3,0,2:T(8,128)(2,1)S(1)} %copy.17), channel_id=1, source_target_pairs={{0,1},{1,2},{2,3},{3,4},{4,5},{5,6},{6,7},{7,8},{8,9},{9,10},{10,1... | collective-permute-start | bytes 589832 | tf_op jit(solution)/shard_map/ppermute | solution.py:57
  632.6 71.9 %collective-permute-start.6 = (bf16[2,384,1,7,128]{4,1,3,0,2:T(8,128)(2,1)}, bf16[2,384,1,7,128]{4,1,3,0,2:T(8,128)(2,1)S(1)}, u32[]{:S(2)}, u32[]{:S(2)}) collective-permute-start(bf16[2,384,1,7,128]{4,1,3,0,2:T(8,128)(2,1)} %get-tuple-element.1072), channel_id=1, source_target_pairs={{0,1},{1,2},{2,3},{3,4},{4,5},{5,6},{6,7},{7,8},{8,9},{9,10},{10,1... | collective-permute-start | bytes 4128776 | tf_op jit(solution)/shard_map/while/body/eval_jaxpr/ppermute | solution.py:57
  634.4 71.2 %collective-permute-start.10 = (bf16[2,384,1,7,128]{4,1,3,0,2:T(8,128)(2,1)}, bf16[2,384,1,7,128]{4,1,3,0,2:T(8,128)(2,1)}, u32[]{:S(2)}, u32[]{:S(2)}) collective-permute-start(bf16[2,384,1,7,128]{4,1,3,0,2:T(8,128)(2,1)} %get-tuple-element.1073), channel_id=1, source_target_pairs={{0,1},{1,2},{2,3},{3,4},{4,5},{5,6},{6,7},{7,8},{8,9},{9,10},{10,1... | collective-permute-start | bytes 4128776 | tf_op jit(solution)/shard_map/while/body/eval_jaxpr/ppermute | solution.py:57
  666.7 54.5 %collective-permute-start.5 = (f32[2,1,384,7,128]{4,2,3,0,1:T(8,128)}, f32[2,1,384,7,128]{4,2,3,0,1:T(8,128)S(1)}, u32[]{:S(2)}, u32[]{:S(2)}) collective-permute-start(f32[2,1,384,7,128]{4,2,3,0,1:T(8,128)} %broadcast_select_fusion.32), channel_id=1, source_target_pairs={{0,1},{1,2},{2,3},{3,4},{4,5},{5,6},{6,7},{7,8},{8,9},{9,10},{10,1... | collective-permute-start | bytes 8257544 | tf_op jit(solution)/shard_map/while/body/eval_jaxpr/ppermute | solution.py:57
  726.4 70.1 %collective-permute-start.6 = (bf16[2,384,1,7,128]{4,1,3,0,2:T(8,128)(2,1)}, bf16[2,384,1,7,128]{4,1,3,0,2:T(8,128)(2,1)S(1)}, u32[]{:S(2)}, u32[]{:S(2)}) collective-permute-start(bf16[2,384,1,7,128]{4,1,3,0,2:T(8,128)(2,1)} %get-tuple-element.1072), channel_id=1, source_target_pairs={{0,1},{1,2},{2,3},{3,4},{4,5},{5,6},{6,7},{7,8},{8,9},{9,10},{10,1... | collective-permute-start | bytes 4128776 | tf_op jit(solution)/shard_map/while/body/eval_jaxpr/ppermute | solution.py:57
  726.4 71.2 %collective-permute-start.10 = (bf16[2,384,1,7,128]{4,1,3,0,2:T(8,128)(2,1)}, bf16[2,384,1,7,128]{4,1,3,0,2:T(8,128)(2,1)}, u32[]{:S(2)}, u32[]{:S(2)}) collective-permute-start(bf16[2,384,1,7,128]{4,1,3,0,2:T(8,128)(2,1)} %get-tuple-element.1073), channel_id=1, source_target_pairs={{0,1},{1,2},{2,3},{3,4},{4,5},{5,6},{6,7},{7,8},{8,9},{9,10},{10,1... | collective-permute-start | bytes 4128776 | tf_op jit(solution)/shard_map/while/body/eval_jaxpr/ppermute | solution.py:57
  758.7 54.5 %collective-permute-start.5 = (f32[2,1,384,7,128]{4,2,3,0,1:T(8,128)}, f32[2,1,384,7,128]{4,2,3,0,1:T(8,128)S(1)}, u32[]{:S(2)}, u32[]{:S(2)}) collective-permute-start(f32[2,1,384,7,128]{4,2,3,0,1:T(8,128)} %broadcast_select_fusion.32), channel_id=1, source_target_pairs={{0,1},{1,2},{2,3},{3,4},{4,5},{5,6},{6,7},{7,8},{8,9},{9,10},{10,1... | collective-permute-start | bytes 8257544 | tf_op jit(solution)/shard_map/while/body/eval_jaxpr/ppermute | solution.py:57
  818.4 72.3 %collective-permute-start.6 = (bf16[2,384,1,7,128]{4,1,3,0,2:T(8,128)(2,1)}, bf16[2,384,1,7,128]{4,1,3,0,2:T(8,128)(2,1)S(1)}, u32[]{:S(2)}, u32[]{:S(2)}) collective-permute-start(bf16[2,384,1,7,128]{4,1,3,0,2:T(8,128)(2,1)} %get-tuple-element.1072), channel_id=1, source_target_pairs={{0,1},{1,2},{2,3},{3,4},{4,5},{5,6},{6,7},{7,8},{8,9},{9,10},{10,1... | collective-permute-start | bytes 4128776 | tf_op jit(solution)/shard_map/while/body/eval_jaxpr/ppermute | solution.py:57
  820.5 71.2 %collective-permute-start.10 = (bf16[2,384,1,7,128]{4,1,3,0,2:T(8,128)(2,1)}, bf16[2,384,1,7,128]{4,1,3,0,2:T(8,128)(2,1)}, u32[]{:S(2)}, u32[]{:S(2)}) collective-permute-start(bf16[2,384,1,7,128]{4,1,3,0,2:T(8,128)(2,1)} %get-tuple-element.1073), channel_id=1, source_target_pairs={{0,1},{1,2},{2,3},{3,4},{4,5},{5,6},{6,7},{7,8},{8,9},{9,10},{10,1... | collective-permute-start | bytes 4128776 | tf_op jit(solution)/shard_map/while/body/eval_jaxpr/ppermute | solution.py:57
  852.9 54.5 %collective-permute-start.5 = (f32[2,1,384,7,128]{4,2,3,0,1:T(8,128)}, f32[2,1,384,7,128]{4,2,3,0,1:T(8,128)S(1)}, u32[]{:S(2)}, u32[]{:S(2)}) collective-permute-start(f32[2,1,384,7,128]{4,2,3,0,1:T(8,128)} %broadcast_select_fusion.32), channel_id=1, source_target_pairs={{0,1},{1,2},{2,3},{3,4},{4,5},{5,6},{6,7},{7,8},{8,9},{9,10},{10,1... | collective-permute-start | bytes 8257544 | tf_op jit(solution)/shard_map/while/body/eval_jaxpr/ppermute | solution.py:57
  912.6 75.5 %collective-permute-start.6 = (bf16[2,384,1,7,128]{4,1,3,0,2:T(8,128)(2,1)}, bf16[2,384,1,7,128]{4,1,3,0,2:T(8,128)(2,1)S(1)}, u32[]{:S(2)}, u32[]{:S(2)}) collective-permute-start(bf16[2,384,1,7,128]{4,1,3,0,2:T(8,128)(2,1)} %get-tuple-element.1072), channel_id=1, source_target_pairs={{0,1},{1,2},{2,3},{3,4},{4,5},{5,6},{6,7},{7,8},{8,9},{9,10},{10,1... | collective-permute-start | bytes 4128776 | tf_op jit(solution)/shard_map/while/body/eval_jaxpr/ppermute | solution.py:57
  918.0 71.2 %collective-permute-start.10 = (bf16[2,384,1,7,128]{4,1,3,0,2:T(8,128)(2,1)}, bf16[2,384,1,7,128]{4,1,3,0,2:T(8,128)(2,1)}, u32[]{:S(2)}, u32[]{:S(2)}) collective-permute-start(bf16[2,384,1,7,128]{4,1,3,0,2:T(8,128)(2,1)} %get-tuple-element.1073), channel_id=1, source_target_pairs={{0,1},{1,2},{2,3},{3,4},{4,5},{5,6},{6,7},{7,8},{8,9},{9,10},{10,1... | collective-permute-start | bytes 4128776 | tf_op jit(solution)/shard_map/while/body/eval_jaxpr/ppermute | solution.py:57
  950.3 54.5 %collective-permute-start.5 = (f32[2,1,384,7,128]{4,2,3,0,1:T(8,128)}, f32[2,1,384,7,128]{4,2,3,0,1:T(8,128)S(1)}, u32[]{:S(2)}, u32[]{:S(2)}) collective-permute-start(f32[2,1,384,7,128]{4,2,3,0,1:T(8,128)} %broadcast_select_fusion.32), channel_id=1, source_target_pairs={{0,1},{1,2},{2,3},{3,4},{4,5},{5,6},{6,7},{7,8},{8,9},{9,10},{10,1... | collective-permute-start | bytes 8257544 | tf_op jit(solution)/shard_map/while/body/eval_jaxpr/ppermute | solution.py:57
  1010.0 75.5 %collective-permute-start.6 = (bf16[2,384,1,7,128]{4,1,3,0,2:T(8,128)(2,1)}, bf16[2,384,1,7,128]{4,1,3,0,2:T(8,128)(2,1)S(1)}, u32[]{:S(2)}, u32[]{:S(2)}) collective-permute-start(bf16[2,384,1,7,128]{4,1,3,0,2:T(8,128)(2,1)} %get-tuple-element.1072), channel_id=1, source_target_pairs={{0,1},{1,2},{2,3},{3,4},{4,5},{5,6},{6,7},{7,8},{8,9},{9,10},{10,1... | collective-permute-start | bytes 4128776 | tf_op jit(solution)/shard_map/while/body/eval_jaxpr/ppermute | solution.py:57
  1015.4 71.2 %collective-permute-start.10 = (bf16[2,384,1,7,128]{4,1,3,0,2:T(8,128)(2,1)}, bf16[2,384,1,7,128]{4,1,3,0,2:T(8,128)(2,1)}, u32[]{:S(2)}, u32[]{:S(2)}) collective-permute-start(bf16[2,384,1,7,128]{4,1,3,0,2:T(8,128)(2,1)} %get-tuple-element.1073), channel_id=1, source_target_pairs={{0,1},{1,2},{2,3},{3,4},{4,5},{5,6},{6,7},{7,8},{8,9},{9,10},{10,1... | collective-permute-start | bytes 4128776 | tf_op jit(solution)/shard_map/while/body/eval_jaxpr/ppermute | solution.py:57
  1047.8 54.5 %collective-permute-start.5 = (f32[2,1,384,7,128]{4,2,3,0,1:T(8,128)}, f32[2,1,384,7,128]{4,2,3,0,1:T(8,128)S(1)}, u32[]{:S(2)}, u32[]{:S(2)}) collective-permute-start(f32[2,1,384,7,128]{4,2,3,0,1:T(8,128)} %broadcast_select_fusion.32), channel_id=1, source_target_pairs={{0,1},{1,2},{2,3},{3,4},{4,5},{5,6},{6,7},{7,8},{8,9},{9,10},{10,1... | collective-permute-start | bytes 8257544 | tf_op jit(solution)/shard_map/while/body/eval_jaxpr/ppermute | solution.py:57
  1107.4 75.5 %collective-permute-start.6 = (bf16[2,384,1,7,128]{4,1,3,0,2:T(8,128)(2,1)}, bf16[2,384,1,7,128]{4,1,3,0,2:T(8,128)(2,1)S(1)}, u32[]{:S(2)}, u32[]{:S(2)}) collective-permute-start(bf16[2,384,1,7,128]{4,1,3,0,2:T(8,128)(2,1)} %get-tuple-element.1072), channel_id=1, source_target_pairs={{0,1},{1,2},{2,3},{3,4},{4,5},{5,6},{6,7},{7,8},{8,9},{9,10},{10,1... | collective-permute-start | bytes 4128776 | tf_op jit(solution)/shard_map/while/body/eval_jaxpr/ppermute | solution.py:57
  1112.8 71.2 %collective-permute-start.10 = (bf16[2,384,1,7,128]{4,1,3,0,2:T(8,128)(2,1)}, bf16[2,384,1,7,128]{4,1,3,0,2:T(8,128)(2,1)}, u32[]{:S(2)}, u32[]{:S(2)}) collective-permute-start(bf16[2,384,1,7,128]{4,1,3,0,2:T(8,128)(2,1)} %get-tuple-element.1073), channel_id=1, source_target_pairs={{0,1},{1,2},{2,3},{3,4},{4,5},{5,6},{6,7},{7,8},{8,9},{9,10},{10,1... | collective-permute-start | bytes 4128776 | tf_op jit(solution)/shard_map/while/body/eval_jaxpr/ppermute | solution.py:57
  1145.2 54.5 %collective-permute-start.5 = (f32[2,1,384,7,128]{4,2,3,0,1:T(8,128)}, f32[2,1,384,7,128]{4,2,3,0,1:T(8,128)S(1)}, u32[]{:S(2)}, u32[]{:S(2)}) collective-permute-start(f32[2,1,384,7,128]{4,2,3,0,1:T(8,128)} %broadcast_select_fusion.32), channel_id=1, source_target_pairs={{0,1},{1,2},{2,3},{3,4},{4,5},{5,6},{6,7},{7,8},{8,9},{9,10},{10,1... | collective-permute-start | bytes 8257544 | tf_op jit(solution)/shard_map/while/body/eval_jaxpr/ppermute | solution.py:57
  1204.9 75.5 %collective-permute-start.6 = (bf16[2,384,1,7,128]{4,1,3,0,2:T(8,128)(2,1)}, bf16[2,384,1,7,128]{4,1,3,0,2:T(8,128)(2,1)S(1)}, u32[]{:S(2)}, u32[]{:S(2)}) collective-permute-start(bf16[2,384,1,7,128]{4,1,3,0,2:T(8,128)(2,1)} %get-tuple-element.1072), channel_id=1, source_target_pairs={{0,1},{1,2},{2,3},{3,4},{4,5},{5,6},{6,7},{7,8},{8,9},{9,10},{10,1... | collective-permute-start | bytes 4128776 | tf_op jit(solution)/shard_map/while/body/eval_jaxpr/ppermute | solution.py:57
  1210.3 71.2 %collective-permute-start.10 = (bf16[2,384,1,7,128]{4,1,3,0,2:T(8,128)(2,1)}, bf16[2,384,1,7,128]{4,1,3,0,2:T(8,128)(2,1)}, u32[]{:S(2)}, u32[]{:S(2)}) collective-permute-start(bf16[2,384,1,7,128]{4,1,3,0,2:T(8,128)(2,1)} %get-tuple-element.1073), channel_id=1, source_target_pairs={{0,1},{1,2},{2,3},{3,4},{4,5},{5,6},{6,7},{7,8},{8,9},{9,10},{10,1... | collective-permute-start | bytes 4128776 | tf_op jit(solution)/shard_map/while/body/eval_jaxpr/ppermute | solution.py:57
  1242.6 54.5 %collective-permute-start.5 = (f32[2,1,384,7,128]{4,2,3,0,1:T(8,128)}, f32[2,1,384,7,128]{4,2,3,0,1:T(8,128)S(1)}, u32[]{:S(2)}, u32[]{:S(2)}) collective-permute-start(f32[2,1,384,7,128]{4,2,3,0,1:T(8,128)} %broadcast_select_fusion.32), channel_id=1, source_target_pairs={{0,1},{1,2},{2,3},{3,4},{4,5},{5,6},{6,7},{7,8},{8,9},{9,10},{10,1... | collective-permute-start | bytes 8257544 | tf_op jit(solution)/shard_map/while/body/eval_jaxpr/ppermute | solution.py:57
  1316.4 152.7 %collective-permute-start.20 = (f32[2,1,384,7,128]{2,4,3,0,1:T(8,128)}, f32[2,1,384,7,128]{2,4,3,0,1:T(8,128)}, u32[]{:S(2)}, u32[]{:S(2)}) collective-permute-start(f32[2,1,384,7,128]{2,4,3,0,1:T(8,128)} %copy.34), channel_id=1, source_target_pairs={{0,9},{1,10},{2,11},{3,12},{4,13},{5,14},{6,15},{7,0},{8,1},{9,2},... | collective-permute-start | bytes 8257544 | tf_op jit(solution)/shard_map/ppermute | solution.py:122
  1326.3 133.7 %collective-permute-start.24 = (f32[2,1,384,128]{3,2,0,1:T(8,128)}, f32[2,1,384,128]{3,2,0,1:T(8,128)}, u32[]{:S(2)}, u32[]{:S(2)}) collective-permute-start(f32[2,1,384,128]{3,2,0,1:T(8,128)} %fusion.102), channel_id=1, source_target_pairs={{0,8},{1,9},{2,10},{3,11},{4,12},{5,13},{6,14},{7,15},{8,0},{9,1},... | collective-permute-start | bytes 1179656 | tf_op jit(solution)/shard_map/ppermute | solution.py:121
  1329.6 138.8 %collective-permute-start.22 = (f32[2,1,384,128]{3,2,0,1:T(8,128)}, f32[2,1,384,128]{3,2,0,1:T(8,128)S(1)}, u32[]{:S(2)}, u32[]{:S(2)}) collective-permute-start(f32[2,1,384,128]{3,2,0,1:T(8,128)} %fusion.106), channel_id=1, source_target_pairs={{0,8},{1,9},{2,10},{3,11},{4,12},{5,13},{6,14},{7,15},{8,0},{9,1},... | collective-permute-start | bytes 1179656 | tf_op jit(solution)/shard_map/ppermute | solution.py:121
  (161 other events, 2451.8 us)
where the time goes:
time: 1490 us; the launch traced here: 1480 us
  waiting for transfers between devices  752 us (50%)
  starting transfers between devices  270 us (18%)
  matrix products  220 us (15%)
  local copies, waits for them, and re-layouts  125 us (8%)
  other arithmetic  108 us (7%)
    ppermute x104, waiting for transfers between devices, send_next(): return lax.ppermute(tree_in, CTX_AXES, next_perm)  538 us
    ppermute x104, starting transfers between devices, send_next(): return lax.ppermute(tree_in, CTX_AXES, next_perm)  247 us
    ppermute x2, waiting for transfers between devices, local_attn(): dk_buf, dv_buf = lax.ppermute((dk_buf, dv_buf), CTX_AXES, home_kv)  130 us
    while x231, local copies, waits for them, and re-layouts  92.9 us
    ppermute x2, waiting for transfers between devices, local_attn(): hlp_out, hlp_lse = lax.ppermute((hlp_out, hlp_lse), CTX_AXES, home_q)  84.1 us
    while x35, other arithmetic  67.2 us
    dot_general x9, matrix products, pair_forward(): jnp.einsum('bhqgk,bkhd->bhqgd', prob_blk.astype(jnp.bfloat16), v_blk, pre...  60.6 us
    dot_general x9, matrix products, pair_backward(): jnp.einsum('bhqgk,bqhgd->bhkd', prob_blk.astype(jnp.bfloat16), do_blk, pr...  46.5 us
  transfers between devices with their start and end apart: 109, of which 32 were waited for; matrix products, arithmetic and copies ran while one was open for 21% of the time, Pallas kernels for 0%

commit v1 on v0

v1 whole, which is shorter than its diff:
```python
import functools
import math

import jax
import jax.numpy as jnp
from jax import lax
from jax.experimental import pallas as pl
from jax.experimental.pallas import tpu as pltpu
from jax.sharding import PartitionSpec as P

MESH = pl.DeviceIdType.MESH
BF = jnp.bfloat16
F32 = jnp.float32


def dot(a, b):
    return jnp.dot(a, b, preferred_element_type=F32)


def kernel(nz, q_in, do_in, k_in, v_in, o_out, dq_out, dk_out, dv_out,
           qs, dos, qT, doT, kvs, kT, vT, oT, dqT, mr, lr, dr, sb, mbr, dkv, ybuf, zbuf, os, dqs, gs,
           in_loc, in_snd, in_rcv, kv_zs, kv_fs, kv_rcv, y_snd, y_rcv, z_snd, z_rcv,
           o_loc, o_snd, o_rcv, g_loc, g_snd, g_rcv, dq_loc, dq_snd, dq_rcv):
    heads, chip_len, dim = qs.shape
    half = chip_len // 2
    tile = min(256, chip_len)
    n_tiles = chip_len // tile
    scale = 1.0 / math.sqrt(dim)
    c2 = scale * math.log2(math.e)

    z = lax.axis_index("ctxo")
    x = lax.axis_index("ctx")
    m = lax.rem(x, 2)
    y = x // 2
    c = 2 * z + y
    peer = {"ctx": 2 * y + 1 - m}
    yn = {"ctx": 2 * (1 - y) + m}
    my_rows = pl.ds(pl.multiple_of(m * half, half), half)
    peer_rows = pl.ds(pl.multiple_of((1 - m) * half, half), half)

    def rcopy(src, dst, ss, rs, dev):
        return pltpu.make_async_remote_copy(src_ref=src, dst_ref=dst, send_sem=ss, recv_sem=rs, device_id=dev, device_id_type=MESH)

    bar = pltpu.get_barrier_semaphore()
    pl.semaphore_signal(bar, inc=1, device_id=peer, device_id_type=MESH)
    pl.semaphore_signal(bar, inc=1, device_id=yn, device_id_type=MESH)
    for d in range(1, nz):
        pl.semaphore_signal(bar, inc=1, device_id={"ctxo": lax.rem(z + d, nz)}, device_id_type=MESH)
    pl.semaphore_wait(bar, nz + 1)

    ins = ((k_in, kvs.at[c, 0]), (v_in, kvs.at[c, 1]), (q_in, qs), (do_in, dos))
    loc, rem = [], []
    for i, (src, dst) in enumerate(ins):
        d = dst.at[my_rows] if i < 2 else dst.at[:, my_rows]
        rem.append(rcopy(src.at[1 - m], d, in_snd.at[i], in_rcv.at[i], peer))
        loc.append(pltpu.make_async_copy(src.at[m], d, in_loc.at[i]))
        rem[-1].start()
        loc[-1].start()
    for i in (0, 1):
        loc[i].wait()
        rem[i].wait_recv()

    def kv_z(t):
        return rcopy(kvs.at[c], kvs.at[c], kv_zs.at[t], kv_rcv.at[c], {"ctxo": t})

    def kv_fwd(p):
        b = 2 * p + y
        return rcopy(kvs.at[b], kvs.at[b], kv_fs.at[p], kv_rcv.at[b], yn)

    def kv_wait(b):
        rcopy(kvs.at[b], kvs.at[b], kv_fs.at[0], kv_rcv.at[b], yn).wait_recv()

    for t in range(nz - 1, 0, -1):
        @pl.when(z < t)
        def _():
            kv_z(t).start()

    @pl.when(y == 0)
    def _():
        kv_fwd(z).start()

    def prep_kv(b):
        kT[b] = kvs[b, 0].T
        vT[b] = kvs[b, 1].T

    prep_kv(c)
    for i in (2, 3):
        loc[i].wait()
        rem[i].wait_recv()

    def prep_q(h, _):
        qT[h] = qs[h].T
        doT[h] = dos[h].T
        return 0

    lax.fori_loop(0, heads, prep_q, 0)

    def tri():
        r = lax.broadcasted_iota(jnp.int32, (tile, tile), 0)
        s = lax.broadcasted_iota(jnp.int32, (tile, tile), 1)
        return s >= r

    def span(t, diag):
        return (t + 1) * tile if diag else chip_len

    def cols(t):
        return slice(t * tile, (t + 1) * tile)

    def masked(s, nk, fill):
        low = jnp.where(tri(), s[nk - tile:], fill)
        return jnp.concatenate([s[:nk - tile], low], axis=0) if nk > tile else low

    def put_scores(t, diag, s):
        nk = span(t, diag)
        if diag:
            s = masked(s, nk, -jnp.inf)
        sb[:nk, cols(t)] = s
        mbr[:, cols(t)] = jnp.max(s, axis=0, keepdims=True)

    def scores(b, h, t, diag):
        return dot(kvs[b, 0, :span(t, diag), :], qT[h, :, cols(t)])

    def fwd_step(b, h, diag, bn, hn, diag_n):
        for t in range(n_tiles):
            sl = cols(t)
            nk = span(t, diag)
            top = mbr[:, sl]
            if not diag:
                old = mr[h, :, sl]
                top = jnp.maximum(old, top)
                fade = jnp.exp2((old - top) * c2)
            s = sb[:nk, sl]
            sn = scores(bn, hn, t, diag_n)
            p = jnp.exp2((s - top) * c2)
            tot = jnp.sum(p, axis=0, keepdims=True)
            o = dot(vT[b, :, :nk], p.astype(BF))
            put_scores(t, diag_n, sn)
            if diag:
                lr[h, :, sl] = tot
                oT[h, :, sl] = o
            else:
                lr[h, :, sl] = lr[h, :, sl] * fade + tot
                oT[h, :, sl] = oT[h, :, sl] * fade + o
            mr[h, :, sl] = top

    def fwd_block(i):
        k = jnp.maximum(i - y, 0)
        p = jnp.maximum(z - 1 - k // 2, 0)
        b = 2 * p + jnp.where(lax.rem(k, 2) == 0, y, 1 - y)
        b = jnp.where(jnp.logical_and(y == 1, i == 0), 2 * z, b)
        return jnp.where(i >= c, c, b)

    def arrive(i):
        k = i - y
        b = fwd_block(i)

        @pl.when(jnp.logical_and(k >= 0, k < 2 * z))
        def _():
            p = z - 1 - k // 2

            @pl.when(jnp.logical_and(k == 0, z > 0))
            def _():
                kv_wait(2 * p + y)
                kv_fwd(p).start()

            @pl.when(lax.rem(k, 2) == 1)
            def _():
                @pl.when(p > 0)
                def _():
                    kv_wait(2 * p - 2 + y)
                    kv_fwd(p - 1).start()

                kv_wait(b)

        @pl.when(jnp.logical_and(k < 0, c > 0))
        def _():
            kv_wait(b)

        @pl.when(i < c)
        def _():
            prep_kv(b)

    for t in range(n_tiles):
        put_scores(t, True, scores(c, 0, t, True))

    def fwd_diag(h, _):
        fwd_step(c, h, True, c, h + 1, True)
        return 0

    lax.fori_loop(0, heads - 1, fwd_diag, 0)
    arrive(0)
    fwd_step(c, heads - 1, True, fwd_block(0), 0, False)

    def fwd_full(n, _):
        i = n // heads
        h = n - i * heads
        last = h == heads - 1

        @pl.when(last)
        def _():
            arrive(i + 1)

        fwd_step(fwd_block(i), h, False, fwd_block(jnp.where(last, i + 1, i)), jnp.where(last, 0, h + 1), False)
        return 0

    lax.fori_loop(0, c * heads, fwd_full, 0)

    def fwd_end(h, _):
        l = lr[h]
        o = oT[h] / l
        mr[h] = mr[h] * c2 + jnp.log2(l)
        dr[h] = jnp.sum(o * doT[h].astype(F32), axis=0, keepdims=True)
        os[h] = o.T.astype(BF)
        dqT[h] = jnp.zeros_like(o)
        return 0

    lax.fori_loop(0, heads, fwd_end, 0)

    def bwd_step(b, h, diag):
        for t in range(n_tiles):
            sl = cols(t)
            nk = span(t, diag)
            s = dot(kvs[b, 0, :nk, :], qT[h, :, sl])
            dp = dot(kvs[b, 1, :nk, :], doT[h, :, sl])
            p = jnp.exp2(s * c2 - mr[h, :, sl])
            if diag:
                p = masked(p, nk, 0.0)
            ds = (p * (dp - dr[h, :, sl])).astype(BF)
            dkv[b, 1, :nk, :] += dot(p.astype(BF), dos[h, sl, :])
            dkv[b, 0, :nk, :] += dot(ds, qs[h, sl, :])
            dqT[h, :, sl] += dot(kT[b, :, :nk], ds)

    def o_copies():
        return (pltpu.make_async_copy(os.at[:, my_rows], o_out.at[m], o_loc),
                rcopy(os.at[:, peer_rows], o_out.at[m], o_snd, o_rcv, peer))

    def bwd_block(i):
        p = i // 2
        b = 2 * p + jnp.where(lax.rem(i, 2) == 0, 1 - y, y)
        return jnp.where(i >= 2 * z, 2 * z, b)

    def y_send(p):
        return rcopy(dkv.at[2 * p + 1 - y], ybuf.at[p], y_snd.at[p], y_rcv.at[p], yn)

    def z_send(p):
        return rcopy(dkv.at[2 * p + y], zbuf.at[z], z_snd.at[p], z_rcv.at[z], {"ctxo": p})

    def y_wait(p):
        rcopy(dkv.at[0], ybuf.at[p], y_snd.at[p], y_rcv.at[p], yn).wait_recv()

    def combine(p):
        y_wait(p)
        dkv[2 * p + y] = dkv[2 * p + y] + ybuf[p]
        z_send(p).start()

    def bwd_full(i, _):
        b = bwd_block(i)
        dkv[b] = jnp.zeros_like(dkv[b])

        def one(h, _):
            bwd_step(b, h, False)
            return 0

        lax.fori_loop(0, heads, one, 0)

        @pl.when(jnp.logical_or(lax.rem(i, 2) == 0, i >= 2 * z))
        def _():
            y_send(i // 2).start()

        @pl.when(jnp.logical_and(lax.rem(i, 2) == 0, i > 0))
        def _():
            combine(i // 2 - 1)

        @pl.when(i == 0)
        def _():
            for cp in o_copies():
                cp.start()

        return 0

    lax.fori_loop(0, c, bwd_full, 0)

    @pl.when(c == 0)
    def _():
        for cp in o_copies():
            cp.start()

    dkv[c] = jnp.zeros_like(dkv[c])

    def dq_copies(h):
        return (pltpu.make_async_copy(dqs.at[h, my_rows], dq_out.at[m, h], dq_loc.at[h]),
                rcopy(dqs.at[h, peer_rows], dq_out.at[m, h], dq_snd.at[h], dq_rcv.at[h], peer))

    def bwd_diag(h, _):
        bwd_step(c, h, True)
        dqs[h] = (dqT[h] * scale).T.astype(BF)

        @pl.when(h > 0)
        def _():
            for cp in dq_copies(h - 1):
                cp.start()

        return 0

    lax.fori_loop(0, heads, bwd_diag, 0)
    for cp in dq_copies(heads - 1):
        cp.start()

    @pl.when(jnp.logical_and(y == 0, z > 0))
    def _():
        combine(z - 1)

    for t in range(nz - 1, 0, -1):
        @pl.when(z < t)
        def _():
            rcopy(dkv.at[0], zbuf.at[t], z_snd.at[0], z_rcv.at[t], {"ctxo": t}).wait_recv()
            dkv[c] = dkv[c] + zbuf[t]

    @pl.when(y == 0)
    def _():
        y_wait(z)
        dkv[c] = dkv[c] + ybuf[z]

    gs[0] = (dkv[c, 0] * scale).astype(BF)
    gs[1] = dkv[c, 1].astype(BF)
    outs = (dk_out, dv_out)
    g_copies = []
    for i in (0, 1):
        g_copies.append((pltpu.make_async_copy(gs.at[i, my_rows], outs[i].at[m], g_loc.at[i]),
                         rcopy(gs.at[i, peer_rows], outs[i].at[m], g_snd.at[i], g_rcv.at[i], peer)))
        for cp in g_copies[-1]:
            cp.start()

    for i in range(4):
        rem[i].wait_send()
    for t in range(1, nz):
        @pl.when(z < t)
        def _():
            kv_z(t).wait_send()
    for p in range(nz):
        @pl.when(jnp.logical_or(p < z, jnp.logical_and(p == z, y == 0)))
        def _():
            kv_fwd(p).wait_send()

        @pl.when(jnp.logical_or(p < z, jnp.logical_and(p == z, y == 1)))
        def _():
            y_send(p).wait_send()

        @pl.when(p < z)
        def _():
            z_send(p).wait_send()
    a, b = o_copies()
    a.wait()
    b.wait()
    for h in range(heads):
        a, b = dq_copies(h)
        a.wait()
        b.wait()
    for a, b in g_copies:
        a.wait()
        b.wait()


def solution(mesh):
    nz = mesh.shape["ctxo"]
    spec = P("data", ("ctxo", "ctx"), None, None)

    def local(q, k, v, do):
        rows, half, heads, dim = q.shape
        n = 2 * half
        nb = 2 * nz
        q, do = jnp.swapaxes(q, 1, 2), jnp.swapaxes(do, 1, 2)
        k, v = k[:, :, 0], v[:, :, 0]
        hbm = pl.BlockSpec(memory_space=pl.ANY)
        dma = pltpu.SemaphoreType.DMA
        S = jax.ShapeDtypeStruct
        V = pltpu.VMEM
        o, dq, dk, dv = pl.pallas_call(
            functools.partial(kernel, nz),
            out_shape=[S(q.shape, BF), S(q.shape, BF), S(k.shape, BF), S(k.shape, BF)],
            in_specs=[hbm] * 4,
            out_specs=[hbm] * 4,
            scratch_shapes=[
                V((heads, n, dim), BF), V((heads, n, dim), BF), V((heads, dim, n), BF), V((heads, dim, n), BF),
                V((nb, 2, n, dim), BF), V((nb, dim, n), BF), V((nb, dim, n), BF),
                V((heads, dim, n), F32), V((heads, dim, n), F32),
                V((heads, 1, n), F32), V((heads, 1, n), F32), V((heads, 1, n), F32),
                V((n, n), F32), V((1, n), F32),
                V((nb, 2, n, dim), F32), V((nz, 2, n, dim), F32), V((nz, 2, n, dim), F32),
                V((heads, n, dim), BF), V((heads, n, dim), BF), V((2, n, dim), BF),
                dma((4,)), dma((4,)), dma((4,)), dma((nz,)), dma((nz,)), dma((nb,)),
                dma((nz,)), dma((nz,)), dma((nz,)), dma((nz,)),
                dma, dma, dma, dma((2,)), dma((2,)), dma((2,)), dma((heads,)), dma((heads,)), dma((heads,)),
            ],
            compiler_params=pltpu.CompilerParams(collective_id=0, has_side_effects=True, vmem_limit_bytes=62 * 1024 * 1024),
            name="attn",
        )(q, do, k, v)
        return jnp.swapaxes(o, 1, 2), jnp.swapaxes(dq, 1, 2), dk[:, :, None], dv[:, :, None]

    return jax.shard_map(local, mesh=mesh, in_specs=(spec,) * 4, out_specs=(spec,) * 4, check_vma=False)
```

time: 1490 us -> 171 us (0.11)
  the two profiles are of different devices: /device:TPU:27 before, /device:TPU:14 now
where the time goes in v1:
time: 171 us; the launch traced here: 170 us
  Pallas kernels  164 us (96%)
  local copies, waits for them, and re-layouts  5.11 us (3%)
    pallas_call x1, Pallas kernels, local(): pl.pallas_call(functools.partial(kernel, nz), out_shape=[S(q.shape, BF),...  164 us
    unnamed x10, local copies, waits for them, and re-layouts  5.11 us

profile of v1, /device:TPU:14, one launch (start us, length us, event | category | flops | bytes accessed | tf_op | source)
XLA Modules:
  0.0 169.5 jit_solution(1728705770943231780)
XLA Ops:
  0.6 163.8 %attn.1 = (bf16[2,7,384,128]{3,2,1,0:T(8,128)(2,1)}, bf16[2,7,384,128]{3,2,1,0:T(8,128)(2,1)}, bf16[2,384,128]{2,1,0:T(8,128)(2,1)}, bf16[2,384,128]{2,1,0:T(8,128)(2,1)}) custom-call(bf16[2,7,384,128]{3,2,1,0:T(8,128)(2,1)} %bitcast.12, bf16[2,7,384,128]{3,2,1,0:T(8,128)(2,1)} %bitcast.13, bf16[2,384,128]{2,1,0:T(8,128)(2,1)} %bitcast.16, ...), custom_call_target="tpu_custom_call" | custom-call | tf_op jit(solution)/shard_map/attn/pallas_call | solution.py:378
  164.4 0.0 copy-start
  164.4 2.6 %copy.14 = bf16[2,384,7,128]{3,1,2,0:T(8,128)(2,1)} copy(bf16[2,384,7,128]{3,1,2,0:T(8,128)(2,1)} %bitcast.15) | data formatting | bytes 2752512
  167.0 0.0 copy-done
  167.0 0.0 copy-start.2
  167.0 0.0 copy-start.1
  167.0 1.1 copy.15
  168.1 0.0 copy-done.2
  168.2 0.7 copy.16
  168.8 0.0 copy-done.1
  168.8 0.7 copy.17
Async XLA Ops:
  164.4 2.6 %copy-start = (bf16[2,7,384,128]{3,2,1,0:T(8,128)(2,1)S(1)}, bf16[2,7,384,128]{3,2,1,0:T(8,128)(2,1)}, u32[]{:S(2)}) copy-start(bf16[2,7,384,128]{3,2,1,0:T(8,128)(2,1)} %get-tuple-element.9) | copy-start | bytes 4128772
  167.0 1.1 copy-start.2
  167.0 1.8 %copy-start.1 = (bf16[2,384,128]{2,1,0:T(8,128)(2,1)S(1)}, bf16[2,384,128]{2,1,0:T(8,128)(2,1)}, u32[]{:S(2)}) copy-start(bf16[2,384,128]{2,1,0:T(8,128)(2,1)} %get-tuple-element.11) | copy-start | bytes 589828

commit v2 on v1

v2 whole, which is shorter than its diff:
```python
import functools
import math

import jax
import jax.numpy as jnp
from jax import lax
from jax.experimental import pallas as pl
from jax.experimental.pallas import tpu as pltpu
from jax.sharding import PartitionSpec as P

MESH = pl.DeviceIdType.MESH
BF = jnp.bfloat16
F32 = jnp.float32
DIAG, SIB, FULL = 0, 1, 2


def dot(a, b):
    return jnp.dot(a, b, preferred_element_type=F32)


def kernel(nz, q_in, do_in, k_in, v_in, o_out, dq_out, dk_out, dv_out,
           qs, dos, qT, doT, kvs, kT, vT, oT, dqT, mr, lr, dr, sb, mbr, dkv, ybuf, zbuf, os, dqs, gs,
           in_loc, in_snd, in_rcv, kv_zs, kv_fs, kv_rcv, y_snd, y_rcv, z_snd, z_rcv,
           o_loc, o_snd, o_rcv, g_loc, g_snd, g_rcv, dq_loc, dq_snd, dq_rcv):
    heads, chip_len, dim = qs.shape
    half = chip_len // 2
    tile = min(256, chip_len)
    n_tiles = chip_len // tile
    scale = 1.0 / math.sqrt(dim)
    c2 = scale * math.log2(math.e)

    z = lax.axis_index("ctxo")
    x = lax.axis_index("ctx")
    m = lax.rem(x, 2)
    y = x // 2
    c = 2 * z + m
    peer = {"ctx": 2 * (1 - y) + m}
    sib = {"ctx": 2 * y + 1 - m}
    my_rows = pl.ds(pl.multiple_of(y * half, half), half)
    peer_rows = pl.ds(pl.multiple_of((1 - y) * half, half), half)

    def rcopy(src, dst, ss, rs, dev):
        return pltpu.make_async_remote_copy(src_ref=src, dst_ref=dst, send_sem=ss, recv_sem=rs, device_id=dev, device_id_type=MESH)

    bar = pltpu.get_barrier_semaphore()
    pl.semaphore_signal(bar, inc=1, device_id=peer, device_id_type=MESH)
    pl.semaphore_signal(bar, inc=1, device_id=sib, device_id_type=MESH)
    for d in range(1, nz):
        pl.semaphore_signal(bar, inc=1, device_id={"ctxo": lax.rem(z + d, nz)}, device_id_type=MESH)
    pl.semaphore_wait(bar, nz + 1)

    rem, loc = [], []
    for i, (src, dst) in enumerate(((k_in, kvs.at[c, 0]), (v_in, kvs.at[c, 1]))):
        rem.append(rcopy(src.at[1 - y], dst.at[my_rows], in_snd.at[i], in_rcv.at[i], peer))
        loc.append(pltpu.make_async_copy(src.at[y], dst.at[my_rows], in_loc.at[i]))
    for h in range(heads):
        rem.append(rcopy(q_in.at[1 - y, h], qs.at[h, my_rows], in_snd.at[2 + h], in_rcv.at[2 + h], peer))
    rem.append(rcopy(do_in.at[1 - y], dos.at[:, my_rows], in_snd.at[2 + heads], in_rcv.at[2 + heads], peer))
    loc.append(pltpu.make_async_copy(q_in.at[y], qs.at[:, my_rows], in_loc.at[2]))
    loc.append(pltpu.make_async_copy(do_in.at[y], dos.at[:, my_rows], in_loc.at[3]))
    for cp in rem:
        cp.start()
    for cp in loc:
        cp.start()
    for i in (0, 1):
        loc[i].wait()
        rem[i].wait_recv()

    def kv_z(t):
        return rcopy(kvs.at[c], kvs.at[c], kv_zs.at[t], kv_rcv.at[c], {"ctxo": t})

    def kv_fwd(p):
        b = 2 * p + m
        return rcopy(kvs.at[b], kvs.at[b], kv_fs.at[p], kv_rcv.at[b], sib)

    def kv_wait(b):
        rcopy(kvs.at[b], kvs.at[b], kv_fs.at[0], kv_rcv.at[b], sib).wait_recv()

    for t in range(nz - 1, 0, -1):
        @pl.when(z < t)
        def _():
            kv_z(t).start()

    kv_fwd(z).start()

    def prep_kv(b):
        kT[b] = kvs[b, 0].T
        vT[b] = kvs[b, 1].T

    prep_kv(c)
    loc[2].wait()

    def prep_q(h):
        rcopy(q_in.at[1 - y, h], qs.at[h, my_rows], in_snd.at[2 + h], in_rcv.at[2 + h], peer).wait_recv()
        qT[h] = qs[h].T

    def tri():
        r = lax.broadcasted_iota(jnp.int32, (tile, tile), 0)
        s = lax.broadcasted_iota(jnp.int32, (tile, tile), 1)
        return s >= r

    def span(t, kind):
        if kind == DIAG:
            return (t + 1) * tile
        return half if kind == SIB and (t + 1) * tile <= half else chip_len

    def cols(t):
        return slice(t * tile, (t + 1) * tile)

    def masked(s, t, kind, fill):
        nk = span(t, kind)
        if kind == DIAG:
            low = jnp.where(tri(), s[nk - tile:], fill)
            return jnp.concatenate([s[:nk - tile], low], axis=0) if nk > tile else low
        if kind == SIB:
            row = lax.broadcasted_iota(jnp.int32, (1, tile), 1) + t * tile
            seen = m * half + jnp.where(row >= half, half, 0)
            return jnp.where(lax.broadcasted_iota(jnp.int32, s.shape, 0) < seen, s, fill)
        return s

    def put_scores(t, kind, s):
        s = masked(s, t, kind, -jnp.inf)
        sb[:span(t, kind), cols(t)] = s
        mbr[:, cols(t)] = jnp.max(s, axis=0, keepdims=True)

    def scores(b, h, t, kind):
        return dot(kvs[b, 0, :span(t, kind), :], qT[h, :, cols(t)])

    def fwd_step(b, h, kind, bn, hn, kind_n):
        for t in range(n_tiles):
            sl = cols(t)
            nk = span(t, kind)
            top = mbr[:, sl]
            if kind != DIAG:
                old = mr[h, :, sl]
                top = jnp.maximum(old, top)
                fade = jnp.exp2((old - top) * c2)
            s = sb[:nk, sl]
            sn = scores(bn, hn, t, kind_n)
            p = jnp.exp2((s - top) * c2)
            tot = jnp.sum(p, axis=0, keepdims=True)
            o = dot(vT[b, :, :nk], p.astype(BF))
            put_scores(t, kind_n, sn)
            if kind == DIAG:
                lr[h, :, sl] = tot
                oT[h, :, sl] = o
            else:
                lr[h, :, sl] = lr[h, :, sl] * fade + tot
                oT[h, :, sl] = oT[h, :, sl] * fade + o
            mr[h, :, sl] = top

    def fwd_block(i):
        b = 2 * (z - 1 - i // 2) + jnp.where(lax.rem(i, 2) == 0, m, 1 - m)
        return jnp.where(i >= 2 * z, c, b)

    def arrive(i):
        b = fwd_block(i)

        @pl.when(i < 2 * z)
        def _():
            kv_wait(b)

            @pl.when(lax.rem(i, 2) == 0)
            def _():
                kv_fwd(z - 1 - i // 2).start()

            prep_kv(b)

    def start_scores(b, h, kind):
        for t in range(n_tiles):
            put_scores(t, kind, scores(b, h, t, kind))

    sb_blk = 2 * z + 1 - m
    prep_q(0)
    start_scores(c, 0, DIAG)
    kv_wait(sb_blk)
    prep_kv(sb_blk)

    def fwd_plane(h, _):
        hn = jnp.minimum(h + 1, heads - 1)

        @pl.when(h + 1 < heads)
        def _():
            prep_q(h + 1)

        fwd_step(c, h, DIAG, sb_blk, h, SIB)
        fwd_step(sb_blk, h, SIB, c, hn, DIAG)
        return 0

    lax.fori_loop(0, heads, fwd_plane, 0)
    arrive(0)
    start_scores(fwd_block(0), 0, FULL)

    def fwd_full(n, _):
        i = n // heads
        h = n - i * heads
        last = h == heads - 1

        @pl.when(last)
        def _():
            arrive(i + 1)

        fwd_step(fwd_block(i), h, FULL, fwd_block(jnp.where(last, i + 1, i)), jnp.where(last, 0, h + 1), FULL)
        return 0

    lax.fori_loop(0, 2 * z * heads, fwd_full, 0)

    loc[3].wait()
    rem[-1].wait_recv()

    def fwd_end(h, _):
        doT[h] = dos[h].T
        l = lr[h]
        o = oT[h] / l
        mr[h] = mr[h] * c2 + jnp.log2(l)
        dr[h] = jnp.sum(o * dos[h].T.astype(F32), axis=0, keepdims=True)
        os[h] = o.T.astype(BF)
        dqT[h] = jnp.zeros_like(o)
        return 0

    lax.fori_loop(0, heads, fwd_end, 0)

    def bwd_step(b, h, kind):
        for t in range(n_tiles):
            sl = cols(t)
            nk = span(t, kind)
            s = dot(kvs[b, 0, :nk, :], qT[h, :, sl])
            dp = dot(kvs[b, 1, :nk, :], doT[h, :, sl])
            p = masked(jnp.exp2(s * c2 - mr[h, :, sl]), t, kind, 0.0)
            ds = (p * (dp - dr[h, :, sl])).astype(BF)
            dkv[b, 1, :nk, :] += dot(p.astype(BF), dos[h, sl, :])
            dkv[b, 0, :nk, :] += dot(ds, qs[h, sl, :])
            dqT[h, :, sl] += dot(kT[b, :, :nk], ds)

    def o_copies():
        return (pltpu.make_async_copy(os.at[:, my_rows], o_out.at[y], o_loc),
                rcopy(os.at[:, peer_rows], o_out.at[y], o_snd, o_rcv, peer))

    def bwd_block(i):
        return i + jnp.where(m == 0, 1 - 2 * lax.rem(i, 2), 0)

    def y_send(p):
        return rcopy(dkv.at[2 * p + 1 - m], ybuf.at[p], y_snd.at[p], y_rcv.at[p], sib)

    def z_send(p):
        return rcopy(dkv.at[2 * p + m], zbuf.at[z], z_snd.at[p], z_rcv.at[z], {"ctxo": p})

    def y_wait(p):
        rcopy(dkv.at[0], ybuf.at[p], y_snd.at[p], y_rcv.at[p], sib).wait_recv()

    def bwd_full(i, _):
        b = bwd_block(i)
        dkv[b] = jnp.zeros_like(dkv[b])

        def one(h, _):
            bwd_step(b, h, FULL)
            return 0

        lax.fori_loop(0, heads, one, 0)
        p = i // 2

        @pl.when(lax.rem(i, 2) == 0)
        def _():
            y_send(p).start()

        @pl.when(lax.rem(i, 2) == 1)
        def _():
            y_wait(p)
            dkv[b] = dkv[b] + ybuf[p]
            z_send(p).start()

        return 0

    for cp in o_copies():
        cp.start()
    lax.fori_loop(0, 2 * z, bwd_full, 0)

    dkv[c] = jnp.zeros_like(dkv[c])
    dkv[sb_blk] = jnp.zeros_like(dkv[sb_blk])

    def dq_copies(h):
        return (pltpu.make_async_copy(dqs.at[h, my_rows], dq_out.at[y, h], dq_loc.at[h]),
                rcopy(dqs.at[h, peer_rows], dq_out.at[y, h], dq_snd.at[h], dq_rcv.at[h], peer))

    def bwd_diag(h, _):
        bwd_step(sb_blk, h, SIB)
        bwd_step(c, h, DIAG)
        dqs[h] = (dqT[h] * scale).T.astype(BF)

        @pl.when(h > 0)
        def _():
            for cp in dq_copies(h - 1):
                cp.start()

        return 0

    lax.fori_loop(0, heads, bwd_diag, 0)
    for cp in dq_copies(heads - 1):
        cp.start()

    y_send(z).start()

    for t in range(nz - 1, 0, -1):
        @pl.when(z < t)
        def _():
            rcopy(dkv.at[0], zbuf.at[t], z_snd.at[0], z_rcv.at[t], {"ctxo": t}).wait_recv()
            dkv[c] = dkv[c] + zbuf[t]

    y_wait(z)
    dkv[c] = dkv[c] + ybuf[z]

    gs[0] = (dkv[c, 0] * scale).astype(BF)
    gs[1] = dkv[c, 1].astype(BF)
    outs = (dk_out, dv_out)
    g_copies = []
    for i in (0, 1):
        g_copies.append((pltpu.make_async_copy(gs.at[i, my_rows], outs[i].at[y], g_loc.at[i]),
                         rcopy(gs.at[i, peer_rows], outs[i].at[y], g_snd.at[i], g_rcv.at[i], peer)))
        for cp in g_copies[-1]:
            cp.start()

    for cp in rem:
        cp.wait_send()
    for t in range(1, nz):
        @pl.when(z < t)
        def _():
            kv_z(t).wait_send()
    for p in range(nz):
        @pl.when(p <= z)
        def _():
            kv_fwd(p).wait_send()
            y_send(p).wait_send()

        @pl.when(p < z)
        def _():
            z_send(p).wait_send()
    a, b = o_copies()
    a.wait()
    b.wait()
    for h in range(heads):
        a, b = dq_copies(h)
        a.wait()
        b.wait()
    for a, b in g_copies:
        a.wait()
        b.wait()


def solution(mesh):
    nz = mesh.shape["ctxo"]
    spec = P("data", ("ctxo", "ctx"), None, None)

    def local(q, k, v, do):
        rows, half, heads, dim = q.shape
        n = 2 * half
        nb = 2 * nz
        q, do = jnp.swapaxes(q, 1, 2), jnp.swapaxes(do, 1, 2)
        k, v = k[:, :, 0], v[:, :, 0]
        hbm = pl.BlockSpec(memory_space=pl.ANY)
        dma = pltpu.SemaphoreType.DMA
        S = jax.ShapeDtypeStruct
        V = pltpu.VMEM
        o, dq, dk, dv = pl.pallas_call(
            functools.partial(kernel, nz),
            out_shape=[S(q.shape, BF), S(q.shape, BF), S(k.shape, BF), S(k.shape, BF)],
            in_specs=[hbm] * 4,
            out_specs=[hbm] * 4,
            scratch_shapes=[
                V((heads, n, dim), BF), V((heads, n, dim), BF), V((heads, dim, n), BF), V((heads, dim, n), BF),
                V((nb, 2, n, dim), BF), V((nb, dim, n), BF), V((nb, dim, n), BF),
                V((heads, dim, n), F32), V((heads, dim, n), F32),
                V((heads, 1, n), F32), V((heads, 1, n), F32), V((heads, 1, n), F32),
                V((n, n), F32), V((1, n), F32),
                V((nb, 2, n, dim), F32), V((nz, 2, n, dim), F32), V((nz, 2, n, dim), F32),
                V((heads, n, dim), BF), V((heads, n, dim), BF), V((2, n, dim), BF),
                dma((4,)), dma((3 + heads,)), dma((3 + heads,)), dma((nz,)), dma((nz,)), dma((nb,)),
                dma((nz,)), dma((nz,)), dma((nz,)), dma((nz,)),
                dma, dma, dma, dma((2,)), dma((2,)), dma((2,)), dma((heads,)), dma((heads,)), dma((heads,)),
            ],
            compiler_params=pltpu.CompilerParams(collective_id=0, has_side_effects=True, vmem_limit_bytes=62 * 1024 * 1024),
            name="attn",
        )(q, do, k, v)
        return jnp.swapaxes(o, 1, 2), jnp.swapaxes(dq, 1, 2), dk[:, :, None], dv[:, :, None]

    return jax.shard_map(local, mesh=mesh, in_specs=(spec,) * 4, out_specs=(spec,) * 4, check_vma=False)
```

time: 171 us -> 163 us (0.953); the launches traced: 170 us -> 163 us
  Pallas kernels: 164 us -> 158 us
    pallas_call x1, Pallas kernels: 164 us -> 158 us  [local(): pl.pallas_call(functools.partial(kernel, nz), out_shape=[S(q.shape, BF),...]
where the time goes in v2:
time: 163 us
  Pallas kernels  158 us (97%)
  local copies, waits for them, and re-layouts  5.11 us (3%)
    pallas_call x1, Pallas kernels, local(): pl.pallas_call(functools.partial(kernel, nz), out_shape=[S(q.shape, BF),...  158 us
    unnamed x10, local copies, waits for them, and re-layouts  5.11 us

profile of v2, /device:TPU:14, one launch (start us, length us, event | category | flops | bytes accessed | tf_op | source)
XLA Modules:
  0.0 163.3 jit_solution(2088965043651361048)
XLA Ops:
  0.6 157.5 %attn.1 = (bf16[2,7,384,128]{3,2,1,0:T(8,128)(2,1)}, bf16[2,7,384,128]{3,2,1,0:T(8,128)(2,1)}, bf16[2,384,128]{2,1,0:T(8,128)(2,1)}, bf16[2,384,128]{2,1,0:T(8,128)(2,1)}) custom-call(bf16[2,7,384,128]{3,2,1,0:T(8,128)(2,1)} %bitcast.12, bf16[2,7,384,128]{3,2,1,0:T(8,128)(2,1)} %bitcast.13, bf16[2,384,128]{2,1,0:T(8,128)(2,1)} %bitcast.16, ...), custom_call_target="tpu_custom_call" | custom-call | tf_op jit(solution)/shard_map/attn/pallas_call | solution.py:363
  158.2 0.0 copy-start
  158.2 2.6 %copy.14 = bf16[2,384,7,128]{3,1,2,0:T(8,128)(2,1)} copy(bf16[2,384,7,128]{3,1,2,0:T(8,128)(2,1)} %bitcast.15) | data formatting | bytes 2752512
  160.8 0.0 copy-done
  160.8 0.0 copy-start.2
  160.8 0.0 copy-start.1
  160.8 1.1 copy.15
  161.9 0.0 copy-done.2
  161.9 0.7 copy.16
  162.6 0.0 copy-done.1
  162.6 0.7 copy.17
Async XLA Ops:
  158.2 2.6 %copy-start = (bf16[2,7,384,128]{3,2,1,0:T(8,128)(2,1)S(1)}, bf16[2,7,384,128]{3,2,1,0:T(8,128)(2,1)}, u32[]{:S(2)}) copy-start(bf16[2,7,384,128]{3,2,1,0:T(8,128)(2,1)} %get-tuple-element.9) | copy-start | bytes 4128772
  160.8 1.1 copy-start.2
  160.8 1.8 %copy-start.1 = (bf16[2,384,128]{2,1,0:T(8,128)(2,1)S(1)}, bf16[2,384,128]{2,1,0:T(8,128)(2,1)}, u32[]{:S(2)}) copy-start(bf16[2,384,128]{2,1,0:T(8,128)(2,1)} %get-tuple-element.11) | copy-start | bytes 589828

commit v3 on v2

v3 whole, which is shorter than its diff:
```python
import functools
import math

import jax
import jax.numpy as jnp
from jax import lax
from jax.experimental import pallas as pl
from jax.experimental.pallas import tpu as pltpu
from jax.sharding import PartitionSpec as P

MESH = pl.DeviceIdType.MESH
BF = jnp.bfloat16
F32 = jnp.float32
DIAG, SIB, FULL = 0, 1, 2
GIVE3, GIVE2 = 2, 0
EXTRA = max(GIVE3, GIVE2)


def dot(a, b):
    return jnp.dot(a, b, preferred_element_type=F32)


def either(*conds):
    return functools.reduce(jnp.logical_or, conds)


def both(*conds):
    return functools.reduce(jnp.logical_and, conds)


def loop(n, body):
    def step(i, carry):
        body(i)
        return carry

    lax.fori_loop(0, n, step, 0)


def kernel(heads, q_in, do_in, k_in, v_in, o_out, dq_out, dk_out, dv_out,
           qs, dos, qT, doT, kvs, kT, vT, oT, dqT, mr, lr, dr, sb, mbr, dkv, ybuf, zbuf, cbuf, os, dqs, gs,
           kv_loc, kv_snd, kv_xrc, qd_loc, q_snd, q_rcv, d_snd, d_rcv, hq_snd, hq_rcv, hd_snd, hd_rcv,
           kv_zs, kv_fs, kv_rcv, y_snd, y_rcv, z_snd, z_rcv, c_rcv,
           o_loc, o_snd, o_rcv, dq_loc, dq_snd, dq_rcv, ho_snd, ho_rcv, hg_snd, hg_rcv, g_loc, g_snd, g_rcv):
    _, chip_len, dim = qs.shape
    nz = 4
    half = chip_len // 2
    tile = min(256, chip_len)
    n_tiles = chip_len // tile
    scale = 1.0 / math.sqrt(dim)
    c2 = scale * math.log2(math.e)

    z = lax.axis_index("ctxo")
    x = lax.axis_index("ctx")
    m = lax.rem(x, 2)
    y = x // 2
    zs = nz - 1 - z
    give = jnp.where(z == 3, GIVE3, jnp.where(z == 2, GIVE2, 0))
    take = jnp.where(z == 0, GIVE3, jnp.where(z == 1, GIVE2, 0))
    n_own = heads - give
    helps = take > 0
    c = 2 * z + m
    peer = {"ctx": 2 * (1 - y) + m}
    sib = {"ctx": 2 * y + 1 - m}
    mates = ({"ctxo": zs}, {"ctxo": zs, "ctx": 2 * (1 - y) + m})
    my_rows = pl.ds(pl.multiple_of(y * half, half), half)
    peer_rows = pl.ds(pl.multiple_of((1 - y) * half, half), half)
    batch = (y, 1 - y)
    rows = (my_rows, peer_rows)

    def rcopy(src, dst, ss, rs, dev):
        return pltpu.make_async_remote_copy(src_ref=src, dst_ref=dst, send_sem=ss, recv_sem=rs, device_id=dev, device_id_type=MESH)

    bar = pltpu.get_barrier_semaphore()
    for dev in (peer, sib, mates[1]) + tuple({"ctxo": lax.rem(z + d, nz)} for d in range(1, nz)):
        pl.semaphore_signal(bar, inc=1, device_id=dev, device_id_type=MESH)
    pl.semaphore_wait(bar, nz + 2)

    def kv_swap(i):
        src = (k_in, v_in)[i]
        return (rcopy(src.at[1 - y], kvs.at[c, i, my_rows], kv_snd.at[i], kv_xrc.at[i], peer),
                pltpu.make_async_copy(src.at[y], kvs.at[c, i, my_rows], kv_loc.at[i]))

    def q_swap(h):
        return rcopy(q_in.at[1 - y, h], qs.at[h, my_rows], q_snd.at[h], q_rcv.at[h], peer)

    def d_swap(h):
        return rcopy(do_in.at[1 - y, h], dos.at[h, my_rows], d_snd.at[h], d_rcv.at[h], peer)

    def q_give(j, r):
        return rcopy(q_in.at[batch[r], jnp.minimum(heads - give + j, heads - 1)], qs.at[heads + j, my_rows], hq_snd.at[j, r], hq_rcv.at[j, r], mates[r])

    def d_give(j, r):
        return rcopy(do_in.at[batch[r], jnp.minimum(heads - give + j, heads - 1)], dos.at[heads + j, my_rows], hd_snd.at[j, r], hd_rcv.at[j, r], mates[r])

    for i in (0, 1):
        for cp in kv_swap(i):
            cp.start()
    loop(n_own, lambda h: q_swap(h).start())
    q_loc = (pltpu.make_async_copy(q_in.at[y], qs.at[:heads, my_rows], qd_loc.at[0]),
             pltpu.make_async_copy(do_in.at[y], dos.at[:heads, my_rows], qd_loc.at[1]))
    for cp in q_loc:
        cp.start()
    dkv[...] = jnp.zeros_like(dkv)
    for i in (0, 1):
        swap, local = kv_swap(i)
        local.wait()
        swap.wait_recv()

    def kv_z(t):
        return rcopy(kvs.at[c], kvs.at[c], kv_zs.at[t], kv_rcv.at[c], {"ctxo": t})

    def kv_goes(t):
        up = z < t
        if t == 0:
            return z > 0 if GIVE3 else z < 0
        if t == 1 and GIVE2:
            return either(up, z == 2)
        return up

    def kv_fwd(p):
        b = 2 * p + m
        return rcopy(kvs.at[b], kvs.at[b], kv_fs.at[p], kv_rcv.at[b], sib)

    def kv_wait(b):
        rcopy(kvs.at[b], kvs.at[b], kv_fs.at[0], kv_rcv.at[b], sib).wait_recv()

    kv_fwd(z).start()
    for t in range(nz - 1, -1, -1):
        @pl.when(kv_goes(t))
        def _():
            kv_z(t).start()

    def give_all(j):
        for r in (0, 1):
            q_give(j, r).start()

    def give_all_d(j):
        for r in (0, 1):
            d_give(j, r).start()

    loop(give, give_all)
    loop(n_own, lambda h: d_swap(h).start())
    loop(give, give_all_d)

    def prep_kv(b):
        kT[b] = kvs[b, 0].T
        vT[b] = kvs[b, 1].T

    prep_kv(c)
    q_loc[0].wait()

    def prep_q(h):
        @pl.when(h < heads)
        def _():
            q_swap(jnp.minimum(h, heads - 1)).wait_recv()

        if EXTRA:
            @pl.when(h >= heads)
            def _():
                for r in (0, 1):
                    q_give(jnp.maximum(h - heads, 0), r).wait_recv()

        qT[h] = qs[h].T

    def tri():
        r = lax.broadcasted_iota(jnp.int32, (tile, tile), 0)
        s = lax.broadcasted_iota(jnp.int32, (tile, tile), 1)
        return s >= r

    def span(t, kind):
        if kind == DIAG:
            return (t + 1) * tile
        return half if kind == SIB and (t + 1) * tile <= half else chip_len

    def cols(t):
        return slice(t * tile, (t + 1) * tile)

    def masked(s, t, kind, fill):
        nk = span(t, kind)
        if kind == DIAG:
            low = jnp.where(tri(), s[nk - tile:], fill)
            return jnp.concatenate([s[:nk - tile], low], axis=0) if nk > tile else low
        if kind == SIB:
            row = lax.broadcasted_iota(jnp.int32, (1, tile), 1) + t * tile
            seen = m * half + jnp.where(row >= half, half, 0)
            return jnp.where(lax.broadcasted_iota(jnp.int32, s.shape, 0) < seen, s, fill)
        return s

    def put_scores(t, kind, s):
        s = masked(s, t, kind, -jnp.inf)
        sb[:span(t, kind), cols(t)] = s
        mbr[:, cols(t)] = jnp.max(s, axis=0, keepdims=True)

    def scores(b, h, t, kind):
        return dot(kvs[b, 0, :span(t, kind), :], qT[h, :, cols(t)])

    def start_scores(b, h, kind):
        for t in range(n_tiles):
            put_scores(t, kind, scores(b, h, t, kind))

    def fwd_step(b, h, kind, bn, hn, kind_n):
        for t in range(n_tiles):
            sl = cols(t)
            nk = span(t, kind)
            top = mbr[:, sl]
            if kind != DIAG:
                old = mr[h, :, sl]
                top = jnp.maximum(old, top)
                fade = jnp.exp2((old - top) * c2)
            s = sb[:nk, sl]
            sn = scores(bn, hn, t, kind_n)
            p = jnp.exp2((s - top) * c2)
            tot = jnp.sum(p, axis=0, keepdims=True)
            o = dot(vT[b, :, :nk], p.astype(BF))
            put_scores(t, kind_n, sn)
            if kind == DIAG:
                lr[h, :, sl] = tot
                oT[h, :, sl] = o
            else:
                lr[h, :, sl] = lr[h, :, sl] * fade + tot
                oT[h, :, sl] = oT[h, :, sl] * fade + o
            mr[h, :, sl] = top

    def fwd_part(part):
        own = part == 0
        zq = jnp.where(own, z, zs)
        h0 = jnp.where(own, 0, heads)
        nh = jnp.where(own, n_own, take)
        cb = 2 * zq + m
        sbk = 2 * zq + 1 - m

        def fwd_block(i):
            b = 2 * (zq - 1 - i // 2) + jnp.where(lax.rem(i, 2) == 0, m, 1 - m)
            return jnp.where(i >= 2 * zq, cb, b)

        def arrive(i):
            b = fwd_block(i)
            p = zq - 1 - i // 2

            @pl.when(both(i < 2 * zq, either(own, p > z)))
            def _():
                kv_wait(b)

                @pl.when(lax.rem(i, 2) == 0)
                def _():
                    kv_fwd(jnp.maximum(p, 0)).start()

                prep_kv(b)

        def plane(n):
            h = h0 + n

            @pl.when(n + 1 < nh)
            def _():
                prep_q(h + 1)

            fwd_step(cb, h, DIAG, sbk, h, SIB)
            fwd_step(sbk, h, SIB, cb, h0 + jnp.minimum(n + 1, nh - 1), DIAG)

        def full(n):
            i = n // nh
            k = n - i * nh
            last = k == nh - 1

            @pl.when(last)
            def _():
                arrive(i + 1)

            fwd_step(fwd_block(i), h0 + k, FULL, fwd_block(jnp.where(last, i + 1, i)), h0 + jnp.where(last, 0, k + 1), FULL)

        @pl.when(nh > 0)
        def _():
            @pl.when(jnp.logical_not(own))
            def _():
                kv_wait(cb)
                kv_fwd(zq).start()
                prep_kv(cb)

            prep_q(h0)
            start_scores(cb, h0, DIAG)
            kv_wait(sbk)
            prep_kv(sbk)
            loop(nh, plane)

            @pl.when(zq > 0)
            def _():
                arrive(0)
                start_scores(fwd_block(0), h0, FULL)
                loop(2 * zq * nh, full)

    loop(2 if EXTRA else 1, fwd_part)

    q_loc[1].wait()

    def slot(n):
        return jnp.where(n < n_own, n, n - n_own + heads)

    def fwd_end(n):
        h = slot(n)

        @pl.when(h < heads)
        def _():
            d_swap(jnp.minimum(h, heads - 1)).wait_recv()

        if EXTRA:
            @pl.when(h >= heads)
            def _():
                for r in (0, 1):
                    d_give(jnp.maximum(h - heads, 0), r).wait_recv()

        d = dos[h].T
        doT[h] = d
        l = lr[h]
        o = oT[h] / l
        mr[h] = mr[h] * c2 + jnp.log2(l)
        dr[h] = jnp.sum(o * d.astype(F32), axis=0, keepdims=True)
        os[h] = o.T.astype(BF)
        dqT[h] = jnp.zeros_like(o)

    loop(n_own + take, fwd_end)

    def res_copies(src, dst, loc, snd, rcv, h):
        return (pltpu.make_async_copy(src.at[h, my_rows], dst.at[y, h], loc.at[h]),
                rcopy(src.at[h, peer_rows], dst.at[y, h], snd.at[h], rcv.at[h], peer))

    def o_copies(h):
        return res_copies(os, o_out, o_loc, o_snd, o_rcv, h)

    def dq_copies(h):
        return res_copies(dqs, dq_out, dq_loc, dq_snd, dq_rcv, h)

    def back(src, dst, snd, rcv, j, r, n):
        return rcopy(src.at[heads + j, rows[r]], dst.at[y, heads - n + j], snd.at[j, r], rcv.at[j, r], mates[r])

    def start_both(pair):
        for cp in pair:
            cp.start()

    loop(n_own, lambda h: start_both(o_copies(h)))
    loop(take, lambda j: start_both(back(os, o_out, ho_snd, ho_rcv, j, r, take) for r in (0, 1)))

    def bwd_step(b, h, kind):
        for t in range(n_tiles):
            sl = cols(t)
            nk = span(t, kind)
            s = dot(kvs[b, 0, :nk, :], qT[h, :, sl])
            dp = dot(kvs[b, 1, :nk, :], doT[h, :, sl])
            p = masked(jnp.exp2(s * c2 - mr[h, :, sl]), t, kind, 0.0)
            ds = (p * (dp - dr[h, :, sl])).astype(BF)
            dkv[b, 1, :nk, :] += dot(p.astype(BF), dos[h, sl, :])
            dkv[b, 0, :nk, :] += dot(ds, qs[h, sl, :])
            dqT[h, :, sl] += dot(kT[b, :, :nk], ds)

    def y_send(p):
        return rcopy(dkv.at[2 * p + 1 - m], ybuf.at[p], y_snd.at[p], y_rcv.at[p], sib)

    def y_add(p):
        rcopy(dkv.at[0], ybuf.at[p], y_snd.at[p], y_rcv.at[p], sib).wait_recv()
        dkv[2 * p + m] = dkv[2 * p + m] + ybuf[p]

    def z_send(p):
        return rcopy(dkv.at[2 * p + m], zbuf.at[z], z_snd.at[p], z_rcv.at[z], {"ctxo": p})

    def c_send(p):
        return rcopy(dkv.at[2 * p + m], cbuf.at[p], z_snd.at[p], c_rcv.at[p], {"ctxo": 2})

    def leave(p):
        @pl.when(both(z == 3, p < 2))
        def _():
            c_send(jnp.minimum(p, 1)).start()

        @pl.when(either(both(z == 3, p == 2), z < 2))
        def _():
            z_send(p).start()

    def chain(p):
        rcopy(dkv.at[0], cbuf.at[p], z_snd.at[p], c_rcv.at[p], {"ctxo": 2}).wait_recv()
        dkv[2 * p + m] = dkv[2 * p + m] + cbuf[p]
        z_send(p).start()

    def finish_dq(h):
        dqs[h] = (dqT[h] * scale).T.astype(BF)

    n_planes = jnp.where(helps, zs, z)

    def bwd_full(i):
        k = i // 2
        p = jnp.where(helps, n_planes - 1 - k, k)
        first = lax.rem(i, 2) == 0
        b = 2 * p + jnp.where(first, 1 - m, m)
        na = jnp.where(p < z, n_own, 0)
        nb = take

        def one(n):
            bwd_step(b, jnp.where(n < na, n, n - na + heads), FULL)

        loop(na + nb, one)

        @pl.when(both(first, p != z))
        def _():
            y_send(p).start()

        if EXTRA:
            @pl.when(both(helps, i == 0))
            def _():
                y_add(zs)
                leave(zs)

        @pl.when(both(jnp.logical_not(first), p != z))
        def _():
            y_add(p)
            leave(p)

        @pl.when(both(z == 2, i == 3))
        def _():
            chain(0)

    def bwd_part(part):
        own = part == 1
        zq = jnp.where(own, z, zs)
        h0 = jnp.where(own, 0, heads)

        def plane(n):
            h = h0 + n
            bwd_step(2 * zq + 1 - m, h, SIB)
            bwd_step(2 * zq + m, h, DIAG)

            @pl.when(own)
            def _():
                finish_dq(h)

                @pl.when(h > 0)
                def _():
                    start_both(dq_copies(jnp.clip(h - 1, 0, heads - 1)))

                @pl.when(both(z == 2, h == 3))
                def _():
                    chain(1)

        loop(jnp.where(own, n_own, take), plane)

        @pl.when(either(own, helps))
        def _():
            y_send(zq).start()

        @pl.when(jnp.logical_not(own))
        def _():
            loop(2 * n_planes, bwd_full)

            def taken_dq(j):
                finish_dq(heads + j)

            loop(take, taken_dq)
            loop(take, lambda j: start_both(back(dqs, dq_out, hg_snd, hg_rcv, j, r, take) for r in (0, 1)))

    loop(2, bwd_part)
    start_both(dq_copies(n_own - 1))

    def z_comes(t):
        if t == 3:
            return z == 2
        if t == 2:
            return z < 2
        if t == 1:
            return either(z == 0, z == 2) if GIVE2 else z == 0
        return z > 0 if GIVE3 else z < 0

    for t in range(nz):
        @pl.when(z_comes(t))
        def _():
            rcopy(dkv.at[0], zbuf.at[t], z_snd.at[0], z_rcv.at[t], {"ctxo": t}).wait_recv()
            dkv[c] = dkv[c] + zbuf[t]

    y_add(z)
    gs[0] = (dkv[c, 0] * scale).astype(BF)
    gs[1] = dkv[c, 1].astype(BF)
    outs = (dk_out, dv_out)
    g_copies = []
    for i in (0, 1):
        g_copies.append((pltpu.make_async_copy(gs.at[i, my_rows], outs[i].at[y], g_loc.at[i]),
                         rcopy(gs.at[i, peer_rows], outs[i].at[y], g_snd.at[i], g_rcv.at[i], peer)))
        start_both(g_copies[-1])

    for i in (0, 1):
        kv_swap(i)[0].wait_send()

    def own_sent(h):
        q_swap(h).wait_send()
        d_swap(h).wait_send()
        for a, b in (o_copies(h), dq_copies(h)):
            a.wait()
            b.wait()

    loop(n_own, own_sent)

    def given(j):
        for r in (0, 1):
            q_give(j, r).wait_send()
            d_give(j, r).wait_send()
            for dst, snd, rcv in ((o_out, ho_snd, ho_rcv), (dq_out, hg_snd, hg_rcv)):
                rcopy(os.at[0, my_rows], dst.at[batch[r], heads - give + j], snd.at[j, r], rcv.at[j, r], mates[r]).wait_recv()

    def taken(j):
        for r in (0, 1):
            back(os, o_out, ho_snd, ho_rcv, j, r, take).wait_send()
            back(dqs, dq_out, hg_snd, hg_rcv, j, r, take).wait_send()

    if EXTRA:
        loop(give, given)
        loop(take, taken)

    for t in range(nz):
        @pl.when(kv_goes(t))
        def _():
            kv_z(t).wait_send()

    def planes_sent(p):
        kv_fwd(p).wait_send()
        y_send(p).wait_send()

        @pl.when(p != z)
        def _():
            z_send(p).wait_send()

    loop(jnp.where(helps, zs, z) + 1, planes_sent)
    for a, b in g_copies:
        a.wait()
        b.wait()


def solution(mesh):
    nz = mesh.shape["ctxo"]
    spec = P("data", ("ctxo", "ctx"), None, None)

    def local(q, k, v, do):
        rows, half, heads, dim = q.shape
        n = 2 * half
        nb = 2 * nz
        nh = heads + EXTRA
        ex = max(EXTRA, 1)
        q, do = jnp.swapaxes(q, 1, 2), jnp.swapaxes(do, 1, 2)
        k, v = k[:, :, 0], v[:, :, 0]
        hbm = pl.BlockSpec(memory_space=pl.ANY)
        S = jax.ShapeDtypeStruct
        V = pltpu.VMEM

        def dma(*shape):
            return pltpu.SemaphoreType.DMA(shape)

        o, dq, dk, dv = pl.pallas_call(
            functools.partial(kernel, heads),
            out_shape=[S(q.shape, BF), S(q.shape, BF), S(k.shape, BF), S(k.shape, BF)],
            in_specs=[hbm] * 4,
            out_specs=[hbm] * 4,
            scratch_shapes=[
                V((nh, n, dim), BF), V((nh, n, dim), BF), V((nh, dim, n), BF), V((nh, dim, n), BF),
                V((nb, 2, n, dim), BF), V((nb, dim, n), BF), V((nb, dim, n), BF),
                V((nh, dim, n), F32), V((nh, dim, n), F32),
                V((nh, 1, n), F32), V((nh, 1, n), F32), V((nh, 1, n), F32),
                V((n, n), F32), V((1, n), F32),
                V((nb, 2, n, dim), F32), V((nz, 2, n, dim), F32), V((nz, 2, n, dim), F32), V((2, 2, n, dim), F32),
                V((nh, n, dim), BF), V((nh, n, dim), BF), V((2, n, dim), BF),
                dma(2), dma(2), dma(2), dma(2), dma(heads), dma(heads), dma(heads), dma(heads),
                dma(ex, 2), dma(ex, 2), dma(ex, 2), dma(ex, 2),
                dma(nz), dma(nz), dma(nb), dma(nz), dma(nz), dma(nz), dma(nz), dma(2),
                dma(heads), dma(heads), dma(heads), dma(heads), dma(heads), dma(heads),
                dma(ex, 2), dma(ex, 2), dma(ex, 2), dma(ex, 2), dma(2), dma(2), dma(2),
            ],
            compiler_params=pltpu.CompilerParams(collective_id=0, has_side_effects=True, vmem_limit_bytes=62 * 1024 * 1024),
            name="attn",
        )(q, do, k, v)
        return jnp.swapaxes(o, 1, 2), jnp.swapaxes(dq, 1, 2), dk[:, :, None], dv[:, :, None]

    return jax.shard_map(local, mesh=mesh, in_specs=(spec,) * 4, out_specs=(spec,) * 4, check_vma=False)
```

time: 163 us -> 156 us (0.957)
  Pallas kernels: 158 us -> 150 us
    pallas_call x1, Pallas kernels: 158 us -> 150 us  [local(): pl.pallas_call(functools.partial(kernel, heads), out_shape=[S(q.shape, BF...]
where the time goes in v3:
time: 156 us
  Pallas kernels  150 us (96%)
  local copies, waits for them, and re-layouts  5.11 us (3%)
    pallas_call x1, Pallas kernels, local(): pl.pallas_call(functools.partial(kernel, heads), out_shape=[S(q.shape, BF...  150 us
    unnamed x10, local copies, waits for them, and re-layouts  5.11 us

profile of v3, /device:TPU:14, one launch (start us, length us, event | category | flops | bytes accessed | tf_op | source)
XLA Modules:
  0.0 155.7 jit_solution(18329505060555591475)
XLA Ops:
  0.6 149.9 %attn.1 = (bf16[2,7,384,128]{3,2,1,0:T(8,128)(2,1)}, bf16[2,7,384,128]{3,2,1,0:T(8,128)(2,1)}, bf16[2,384,128]{2,1,0:T(8,128)(2,1)}, bf16[2,384,128]{2,1,0:T(8,128)(2,1)}) custom-call(bf16[2,7,384,128]{3,2,1,0:T(8,128)(2,1)} %bitcast.12, bf16[2,7,384,128]{3,2,1,0:T(8,128)(2,1)} %bitcast.13, bf16[2,384,128]{2,1,0:T(8,128)(2,1)} %bitcast.16, ...), custom_call_target="tpu_custom_call" | custom-call | tf_op jit(solution)/shard_map/attn/pallas_call | solution.py:550
  150.5 0.0 copy-start
  150.6 2.6 %copy.14 = bf16[2,384,7,128]{3,1,2,0:T(8,128)(2,1)} copy(bf16[2,384,7,128]{3,1,2,0:T(8,128)(2,1)} %bitcast.15) | data formatting | bytes 2752512
  153.2 0.0 copy-done
  153.2 0.0 copy-start.2
  153.2 0.0 copy-start.1
  153.2 1.1 copy.15
  154.3 0.0 copy-done.2
  154.3 0.7 copy.16
  155.0 0.0 copy-done.1
  155.0 0.7 copy.17
Async XLA Ops:
  150.5 2.6 %copy-start = (bf16[2,7,384,128]{3,2,1,0:T(8,128)(2,1)S(1)}, bf16[2,7,384,128]{3,2,1,0:T(8,128)(2,1)}, u32[]{:S(2)}) copy-start(bf16[2,7,384,128]{3,2,1,0:T(8,128)(2,1)} %get-tuple-element.9) | copy-start | bytes 4128772
  153.2 1.1 copy-start.2
  153.2 1.8 %copy-start.1 = (bf16[2,384,128]{2,1,0:T(8,128)(2,1)S(1)}, bf16[2,384,128]{2,1,0:T(8,128)(2,1)}, u32[]{:S(2)}) copy-start(bf16[2,384,128]{2,1,0:T(8,128)(2,1)} %get-tuple-element.11) | copy-start | bytes 589828

commit v4 on v3

--- a/solution.py
+++ b/solution.py
@@ -95,7 +95,6 @@
     for i in (0, 1):
         for cp in kv_swap(i):
             cp.start()
-    loop(n_own, lambda h: q_swap(h).start())
     q_loc = (pltpu.make_async_copy(q_in.at[y], qs.at[:heads, my_rows], qd_loc.at[0]),
              pltpu.make_async_copy(do_in.at[y], dos.at[:heads, my_rows], qd_loc.at[1]))
     for cp in q_loc:
@@ -105,6 +104,7 @@
         swap, local = kv_swap(i)
         local.wait()
         swap.wait_recv()
+    loop(n_own, lambda h: q_swap(h).start())
 
     def kv_z(t):
         return rcopy(kvs.at[c], kvs.at[c], kv_zs.at[t], kv_rcv.at[c], {"ctxo": t})
@@ -411,7 +411,7 @@
             y_add(p)
             leave(p)
 
-        @pl.when(both(z == 2, i == 3))
+        @pl.when(both(z == 2, i == 2))
         def _():
             chain(0)
 
@@ -433,7 +433,7 @@
                 def _():
                     start_both(dq_copies(jnp.clip(h - 1, 0, heads - 1)))
 
-                @pl.when(both(z == 2, h == 3))
+                @pl.when(both(z == 2, h == 1))
                 def _():
                     chain(1)
 

time: 156 us -> 146 us (0.936)
  Pallas kernels: 150 us -> 140 us
    pallas_call x1, Pallas kernels: 150 us -> 140 us  [local(): pl.pallas_call(functools.partial(kernel, heads), out_shape=[S(q.shape, BF...]
where the time goes in v4:
time: 146 us
  Pallas kernels  140 us (96%)
  local copies, waits for them, and re-layouts  5.11 us (4%)
    pallas_call x1, Pallas kernels, local(): pl.pallas_call(functools.partial(kernel, heads), out_shape=[S(q.shape, BF...  140 us
    unnamed x10, local copies, waits for them, and re-layouts  5.11 us

profile of v4, /device:TPU:14, one launch (start us, length us, event | category | flops | bytes accessed | tf_op | source)
XLA Modules:
  0.0 145.8 jit_solution(575317438010315550)
XLA Ops:
  0.6 140.0 %attn.1 = (bf16[2,7,384,128]{3,2,1,0:T(8,128)(2,1)}, bf16[2,7,384,128]{3,2,1,0:T(8,128)(2,1)}, bf16[2,384,128]{2,1,0:T(8,128)(2,1)}, bf16[2,384,128]{2,1,0:T(8,128)(2,1)}) custom-call(bf16[2,7,384,128]{3,2,1,0:T(8,128)(2,1)} %bitcast.12, bf16[2,7,384,128]{3,2,1,0:T(8,128)(2,1)} %bitcast.13, bf16[2,384,128]{2,1,0:T(8,128)(2,1)} %bitcast.16, ...), custom_call_target="tpu_custom_call" | custom-call | tf_op jit(solution)/shard_map/attn/pallas_call | solution.py:550
  140.6 0.0 copy-start
  140.7 2.6 %copy.14 = bf16[2,384,7,128]{3,1,2,0:T(8,128)(2,1)} copy(bf16[2,384,7,128]{3,1,2,0:T(8,128)(2,1)} %bitcast.15) | data formatting | bytes 2752512
  143.3 0.0 copy-done
  143.3 0.0 copy-start.2
  143.3 0.0 copy-start.1
  143.3 1.1 copy.15
  144.4 0.0 copy-done.2
  144.4 0.7 copy.16
  145.1 0.0 copy-done.1
  145.1 0.7 copy.17
Async XLA Ops:
  140.6 2.6 %copy-start = (bf16[2,7,384,128]{3,2,1,0:T(8,128)(2,1)S(1)}, bf16[2,7,384,128]{3,2,1,0:T(8,128)(2,1)}, u32[]{:S(2)}) copy-start(bf16[2,7,384,128]{3,2,1,0:T(8,128)(2,1)} %get-tuple-element.9) | copy-start | bytes 4128772
  143.3 1.1 copy-start.2
  143.3 1.8 %copy-start.1 = (bf16[2,384,128]{2,1,0:T(8,128)(2,1)S(1)}, bf16[2,384,128]{2,1,0:T(8,128)(2,1)}, u32[]{:S(2)}) copy-start(bf16[2,384,128]{2,1,0:T(8,128)(2,1)} %get-tuple-element.11) | copy-start | bytes 589828

commit v5 on v4

--- a/solution.py
+++ b/solution.py
@@ -14,6 +14,7 @@
 DIAG, SIB, FULL = 0, 1, 2
 GIVE3, GIVE2 = 2, 0
 EXTRA = max(GIVE3, GIVE2)
+RELAY1, RELAY2 = 3, 4
 
 
 def dot(a, b):
@@ -39,7 +40,7 @@
 def kernel(heads, q_in, do_in, k_in, v_in, o_out, dq_out, dk_out, dv_out,
            qs, dos, qT, doT, kvs, kT, vT, oT, dqT, mr, lr, dr, sb, mbr, dkv, ybuf, zbuf, cbuf, os, dqs, gs,
            kv_loc, kv_snd, kv_xrc, qd_loc, q_snd, q_rcv, d_snd, d_rcv, hq_snd, hq_rcv, hd_snd, hd_rcv,
-           kv_zs, kv_fs, kv_rcv, y_snd, y_rcv, z_snd, z_rcv, c_rcv,
+           kv_us, kv_ds, kv_fs, kv_rcv, y_snd, y_rcv, z_snd, z_rcv, c_rcv,
            o_loc, o_snd, o_rcv, dq_loc, dq_snd, dq_rcv, ho_snd, ho_rcv, hg_snd, hg_rcv, g_loc, g_snd, g_rcv):
     _, chip_len, dim = qs.shape
     nz = 4
@@ -104,18 +105,16 @@
         swap, local = kv_swap(i)
         local.wait()
         swap.wait_recv()
-    loop(n_own, lambda h: q_swap(h).start())
-
-    def kv_z(t):
-        return rcopy(kvs.at[c], kvs.at[c], kv_zs.at[t], kv_rcv.at[c], {"ctxo": t})
-
-    def kv_goes(t):
-        up = z < t
-        if t == 0:
-            return z > 0 if GIVE3 else z < 0
-        if t == 1 and GIVE2:
-            return either(up, z == 2)
-        return up
+    for h in (0, 1):
+        q_swap(h).start()
+
+    def kv_up(p):
+        b = 2 * p + m
+        return rcopy(kvs.at[b], kvs.at[b], kv_us.at[p], kv_rcv.at[b], {"ctxo": jnp.minimum(z + 1, nz - 1)})
+
+    def kv_down(p):
+        b = 2 * p + m
+        return rcopy(kvs.at[b], kvs.at[b], kv_ds.at[p], kv_rcv.at[b], {"ctxo": jnp.maximum(z - 1, 0)})
 
     def kv_fwd(p):
         b = 2 * p + m
@@ -125,10 +124,38 @@
         rcopy(kvs.at[b], kvs.at[b], kv_fs.at[0], kv_rcv.at[b], sib).wait_recv()
 
     kv_fwd(z).start()
-    for t in range(nz - 1, -1, -1):
-        @pl.when(kv_goes(t))
-        def _():
-            kv_z(t).start()
+    @pl.when(z < nz - 1)
+    def _():
+        kv_up(z).start()
+
+    if EXTRA:
+        @pl.when(z > 0)
+        def _():
+            kv_down(z).start()
+
+    between = both(z > 0, z < nz - 1)
+
+    def relay(r):
+        lo, hi = z - r, z + r
+
+        @pl.when(both(between, lo >= 0))
+        def _():
+            p = jnp.maximum(lo, 0)
+            kv_wait(2 * p + m)
+            kv_up(p).start()
+            kv_fwd(p).start()
+
+        if EXTRA:
+            @pl.when(both(between, hi < nz))
+            def _():
+                p = jnp.minimum(hi, nz - 1)
+                kv_wait(2 * p + m)
+                kv_down(p).start()
+
+                if GIVE2:
+                    @pl.when(both(z == 1, r == 1))
+                    def _():
+                        kv_fwd(p).start()
 
     def give_all(j):
         for r in (0, 1):
@@ -138,10 +165,6 @@
         for r in (0, 1):
             d_give(j, r).start()
 
-    loop(give, give_all)
-    loop(n_own, lambda h: d_swap(h).start())
-    loop(give, give_all_d)
-
     def prep_kv(b):
         kT[b] = kvs[b, 0].T
         vT[b] = kvs[b, 1].T
@@ -153,6 +176,14 @@
         @pl.when(h < heads)
         def _():
             q_swap(jnp.minimum(h, heads - 1)).wait_recv()
+
+            @pl.when(h + 2 < n_own)
+            def _():
+                q_swap(jnp.minimum(h + 2, heads - 1)).start()
+
+            @pl.when(h + 2 == n_own)
+            def _():
+                loop(n_own, lambda k: d_swap(k).start())
 
         if EXTRA:
             @pl.when(h >= heads)
@@ -239,9 +270,13 @@
 
             @pl.when(both(i < 2 * zq, either(own, p > z)))
             def _():
-                kv_wait(b)
-
-                @pl.when(lax.rem(i, 2) == 0)
+                column = lax.rem(i, 2) == 0
+
+                @pl.when(jnp.logical_not(both(between, column)))
+                def _():
+                    kv_wait(b)
+
+                @pl.when(both(jnp.logical_not(between), column))
                 def _():
                     kv_fwd(jnp.maximum(p, 0)).start()
 
@@ -253,6 +288,19 @@
             @pl.when(n + 1 < nh)
             def _():
                 prep_q(h + 1)
+
+            @pl.when(both(own, n == RELAY1))
+            def _():
+                relay(1)
+
+            if EXTRA:
+                @pl.when(both(own, n == RELAY1))
+                def _():
+                    loop(give, give_all)
+
+                @pl.when(both(own, n == n_own - 1))
+                def _():
+                    loop(give, give_all_d)
 
             fwd_step(cb, h, DIAG, sbk, h, SIB)
             fwd_step(sbk, h, SIB, cb, h0 + jnp.minimum(n + 1, nh - 1), DIAG)
@@ -262,6 +310,10 @@
             k = n - i * nh
             last = k == nh - 1
 
+            @pl.when(both(own, n == RELAY2))
+            def _():
+                relay(2)
+
             @pl.when(last)
             def _():
                 arrive(i + 1)
@@ -272,8 +324,11 @@
         def _():
             @pl.when(jnp.logical_not(own))
             def _():
-                kv_wait(cb)
-                kv_fwd(zq).start()
+                @pl.when(jnp.logical_not(between))
+                def _():
+                    kv_wait(cb)
+                    kv_fwd(zq).start()
+
                 prep_kv(cb)
 
             prep_q(h0)
@@ -509,10 +564,14 @@
         loop(give, given)
         loop(take, taken)
 
-    for t in range(nz):
-        @pl.when(kv_goes(t))
-        def _():
-            kv_z(t).wait_send()
+    @pl.when(z < nz - 1)
+    def _():
+        loop(z + 1, lambda p: kv_up(p).wait_send())
+
+    if EXTRA:
+        @pl.when(z > 0)
+        def _():
+            loop(nz - z, lambda k: kv_down(z + k).wait_send())
 
     def planes_sent(p):
         kv_fwd(p).wait_send()
@@ -562,7 +621,7 @@
                 V((nh, n, dim), BF), V((nh, n, dim), BF), V((2, n, dim), BF),
                 dma(2), dma(2), dma(2), dma(2), dma(heads), dma(heads), dma(heads), dma(heads),
                 dma(ex, 2), dma(ex, 2), dma(ex, 2), dma(ex, 2),
-                dma(nz), dma(nz), dma(nb), dma(nz), dma(nz), dma(nz), dma(nz), dma(2),
+                dma(nz), dma(nz), dma(nz), dma(nb), dma(nz), dma(nz), dma(nz), dma(nz), dma(2),
                 dma(heads), dma(heads), dma(heads), dma(heads), dma(heads), dma(heads),
                 dma(ex, 2), dma(ex, 2), dma(ex, 2), dma(ex, 2), dma(2), dma(2), dma(2),
             ],

time: 146 us -> 148 us (1.014)
  the two profiles are of different devices: /device:TPU:14 before, /device:TPU:0 now
where the time goes in v5:
time: 148 us
  Pallas kernels  142 us (96%)
  local copies, waits for them, and re-layouts  5.11 us (3%)
    pallas_call x1, Pallas kernels, local(): pl.pallas_call(functools.partial(kernel, heads), out_shape=[S(q.shape, BF...  142 us
    unnamed x10, local copies, waits for them, and re-layouts  5.11 us

profile of v5, /device:TPU:0, one launch (start us, length us, event | category | flops | bytes accessed | tf_op | source)
XLA Modules:
  0.0 148.1 jit_solution(4932864254976840351)
XLA Ops:
  0.6 142.3 %attn.1 = (bf16[2,7,384,128]{3,2,1,0:T(8,128)(2,1)}, bf16[2,7,384,128]{3,2,1,0:T(8,128)(2,1)}, bf16[2,384,128]{2,1,0:T(8,128)(2,1)}, bf16[2,384,128]{2,1,0:T(8,128)(2,1)}) custom-call(bf16[2,7,384,128]{3,2,1,0:T(8,128)(2,1)} %bitcast.12, bf16[2,7,384,128]{3,2,1,0:T(8,128)(2,1)} %bitcast.13, bf16[2,384,128]{2,1,0:T(8,128)(2,1)} %bitcast.16, ...), custom_call_target="tpu_custom_call" | custom-call | tf_op jit(solution)/shard_map/attn/pallas_call | solution.py:609
  142.9 0.0 copy-start
  143.0 2.6 %copy.14 = bf16[2,384,7,128]{3,1,2,0:T(8,128)(2,1)} copy(bf16[2,384,7,128]{3,1,2,0:T(8,128)(2,1)} %bitcast.15) | data formatting | bytes 2752512
  145.6 0.0 copy-done
  145.6 0.0 copy-start.2
  145.6 0.0 copy-start.1
  145.6 1.1 copy.15
  146.7 0.0 copy-done.2
  146.7 0.7 copy.16
  147.4 0.0 copy-done.1
  147.4 0.7 copy.17
Async XLA Ops:
  142.9 2.6 %copy-start = (bf16[2,7,384,128]{3,2,1,0:T(8,128)(2,1)S(1)}, bf16[2,7,384,128]{3,2,1,0:T(8,128)(2,1)}, u32[]{:S(2)}) copy-start(bf16[2,7,384,128]{3,2,1,0:T(8,128)(2,1)} %get-tuple-element.9) | copy-start | bytes 4128772
  145.6 1.1 copy-start.2
  145.6 1.8 %copy-start.1 = (bf16[2,384,128]{2,1,0:T(8,128)(2,1)S(1)}, bf16[2,384,128]{2,1,0:T(8,128)(2,1)}, u32[]{:S(2)}) copy-start(bf16[2,384,128]{2,1,0:T(8,128)(2,1)} %get-tuple-element.11) | copy-start | bytes 589828

commit v6 on v5

--- a/solution.py
+++ b/solution.py
@@ -12,8 +12,7 @@
 BF = jnp.bfloat16
 F32 = jnp.float32
 DIAG, SIB, FULL = 0, 1, 2
-GIVE3, GIVE2 = 2, 0
-EXTRA = max(GIVE3, GIVE2)
+EXTRA = 2
 RELAY1, RELAY2 = 3, 4
 
 
@@ -54,9 +53,9 @@
     x = lax.axis_index("ctx")
     m = lax.rem(x, 2)
     y = x // 2
-    zs = nz - 1 - z
-    give = jnp.where(z == 3, GIVE3, jnp.where(z == 2, GIVE2, 0))
-    take = jnp.where(z == 0, GIVE3, jnp.where(z == 1, GIVE2, 0))
+    zs = lax.rem(z + 2, nz)
+    give = jnp.where(z == 3, EXTRA, 0)
+    take = jnp.where(z == 1, EXTRA, 0)
     n_own = heads - give
     helps = take > 0
     c = 2 * z + m
@@ -129,7 +128,7 @@
         kv_up(z).start()
 
     if EXTRA:
-        @pl.when(z > 0)
+        @pl.when(z >= 2)
         def _():
             kv_down(z).start()
 
@@ -146,16 +145,11 @@
             kv_fwd(p).start()
 
         if EXTRA:
-            @pl.when(both(between, hi < nz))
+            @pl.when(both(z == 2, hi < nz))
             def _():
                 p = jnp.minimum(hi, nz - 1)
                 kv_wait(2 * p + m)
                 kv_down(p).start()
-
-                if GIVE2:
-                    @pl.when(both(z == 1, r == 1))
-                    def _():
-                        kv_fwd(p).start()
 
     def give_all(j):
         for r in (0, 1):
@@ -271,12 +265,13 @@
             @pl.when(both(i < 2 * zq, either(own, p > z)))
             def _():
                 column = lax.rem(i, 2) == 0
-
-                @pl.when(jnp.logical_not(both(between, column)))
+                relayed = both(between, column, p < z)
+
+                @pl.when(jnp.logical_not(relayed))
                 def _():
                     kv_wait(b)
 
-                @pl.when(both(jnp.logical_not(between), column))
+                @pl.when(both(jnp.logical_not(relayed), column))
                 def _():
                     kv_fwd(jnp.maximum(p, 0)).start()
 
@@ -324,11 +319,8 @@
         def _():
             @pl.when(jnp.logical_not(own))
             def _():
-                @pl.when(jnp.logical_not(between))
-                def _():
-                    kv_wait(cb)
-                    kv_fwd(zq).start()
-
+                kv_wait(cb)
+                kv_fwd(zq).start()
                 prep_kv(cb)
 
             prep_q(h0)
@@ -517,8 +509,8 @@
         if t == 2:
             return z < 2
         if t == 1:
-            return either(z == 0, z == 2) if GIVE2 else z == 0
-        return z > 0 if GIVE3 else z < 0
+            return z != 1 if EXTRA else z == 0
+        return z < 0
 
     for t in range(nz):
         @pl.when(z_comes(t))
@@ -569,7 +561,7 @@
         loop(z + 1, lambda p: kv_up(p).wait_send())
 
     if EXTRA:
-        @pl.when(z > 0)
+        @pl.when(z >= 2)
         def _():
             loop(nz - z, lambda k: kv_down(z + k).wait_send())
 

time: 148 us -> 144 us (0.973)
  the two profiles are of different devices: /device:TPU:0 before, /device:TPU:14 now
where the time goes in v6:
time: 144 us; the launch traced here: 142 us
  Pallas kernels  137 us (95%)
  local copies, waits for them, and re-layouts  5.11 us (4%)
    pallas_call x1, Pallas kernels, local(): pl.pallas_call(functools.partial(kernel, heads), out_shape=[S(q.shape, BF...  137 us
    unnamed x10, local copies, waits for them, and re-layouts  5.11 us

profile of v6, /device:TPU:14, one launch (start us, length us, event | category | flops | bytes accessed | tf_op | source)
XLA Modules:
  0.0 142.4 jit_solution(13175599438077257141)
XLA Ops:
  0.6 136.6 %attn.1 = (bf16[2,7,384,128]{3,2,1,0:T(8,128)(2,1)}, bf16[2,7,384,128]{3,2,1,0:T(8,128)(2,1)}, bf16[2,384,128]{2,1,0:T(8,128)(2,1)}, bf16[2,384,128]{2,1,0:T(8,128)(2,1)}) custom-call(bf16[2,7,384,128]{3,2,1,0:T(8,128)(2,1)} %bitcast.12, bf16[2,7,384,128]{3,2,1,0:T(8,128)(2,1)} %bitcast.13, bf16[2,384,128]{2,1,0:T(8,128)(2,1)} %bitcast.16, ...), custom_call_target="tpu_custom_call" | custom-call | tf_op jit(solution)/shard_map/attn/pallas_call | solution.py:601
  137.2 0.0 copy-start
  137.3 2.6 %copy.14 = bf16[2,384,7,128]{3,1,2,0:T(8,128)(2,1)} copy(bf16[2,384,7,128]{3,1,2,0:T(8,128)(2,1)} %bitcast.15) | data formatting | bytes 2752512
  139.9 0.0 copy-done
  139.9 0.0 copy-start.2
  139.9 0.0 copy-start.1
  139.9 1.1 copy.15
  141.0 0.0 copy-done.2
  141.0 0.7 copy.16
  141.7 0.0 copy-done.1
  141.7 0.7 copy.17
Async XLA Ops:
  137.2 2.6 %copy-start = (bf16[2,7,384,128]{3,2,1,0:T(8,128)(2,1)S(1)}, bf16[2,7,384,128]{3,2,1,0:T(8,128)(2,1)}, u32[]{:S(2)}) copy-start(bf16[2,7,384,128]{3,2,1,0:T(8,128)(2,1)} %get-tuple-element.9) | copy-start | bytes 4128772
  139.9 1.1 copy-start.2
  139.9 1.8 %copy-start.1 = (bf16[2,384,128]{2,1,0:T(8,128)(2,1)S(1)}, bf16[2,384,128]{2,1,0:T(8,128)(2,1)}, u32[]{:S(2)}) copy-start(bf16[2,384,128]{2,1,0:T(8,128)(2,1)} %get-tuple-element.11) | copy-start | bytes 589828

commit v7 on v6

--- a/solution.py
+++ b/solution.py
@@ -12,7 +12,7 @@
 BF = jnp.bfloat16
 F32 = jnp.float32
 DIAG, SIB, FULL = 0, 1, 2
-EXTRA = 2
+EXTRA = 1
 RELAY1, RELAY2 = 3, 4
 
 
@@ -432,7 +432,7 @@
 
     def bwd_full(i):
         k = i // 2
-        p = jnp.where(helps, n_planes - 1 - k, k)
+        p = jnp.where(helps, jnp.where(k == 0, 2, k - 1), k)
         first = lax.rem(i, 2) == 0
         b = 2 * p + jnp.where(first, 1 - m, m)
         na = jnp.where(p < z, n_own, 0)
@@ -577,6 +577,20 @@
     for a, b in g_copies:
         a.wait()
         b.wait()
+
+
+def hand_over(*refs):
+    srcs, dsts, bufs, came, left = refs[:4], refs[4:8], refs[8:12], refs[12], refs[13]
+    parts = [(i, b) for i in range(4) for b in range(srcs[0].shape[0])]
+    ins = [pltpu.make_async_copy(srcs[i].at[b], bufs[i].at[b], came.at[n]) for n, (i, b) in enumerate(parts)]
+    outs = [pltpu.make_async_copy(bufs[i].at[b], dsts[i].at[b], left.at[n]) for n, (i, b) in enumerate(parts)]
+    for cp in ins:
+        cp.start()
+    for a, b in zip(ins, outs):
+        a.wait()
+        b.start()
+    for cp in outs:
+        cp.wait()
 
 
 def solution(mesh):
@@ -620,6 +634,14 @@
             compiler_params=pltpu.CompilerParams(collective_id=0, has_side_effects=True, vmem_limit_bytes=62 * 1024 * 1024),
             name="attn",
         )(q, do, k, v)
+        o, dq, dk, dv = pl.pallas_call(
+            hand_over,
+            out_shape=[S(t.shape, BF) for t in (o, dq, dk, dv)],
+            in_specs=[hbm] * 4,
+            out_specs=[hbm] * 4,
+            scratch_shapes=[V(t.shape, BF) for t in (o, dq, dk, dv)] + [dma(4 * rows), dma(4 * rows)],
+            name="hand_over",
+        )(o, dq, dk, dv)
         return jnp.swapaxes(o, 1, 2), jnp.swapaxes(dq, 1, 2), dk[:, :, None], dv[:, :, None]
 
     return jax.shard_map(local, mesh=mesh, in_specs=(spec,) * 4, out_specs=(spec,) * 4, check_vma=False)

time: 144 us -> 140 us (0.972)
  the two profiles are of different devices: /device:TPU:14 before, /device:TPU:26 now
where the time goes in v7:
time: 140 us
  Pallas kernels  140 us (100%)
    pallas_call x1, Pallas kernels, local(): pl.pallas_call(functools.partial(kernel, heads), out_shape=[S(q.shape, BF...  137 us
    pallas_call x1, Pallas kernels, local(): pl.pallas_call(hand_over, out_shape=[S(t.shape, BF) for t in (o, dq, dk,...  2.88 us

profile of v7, /device:TPU:26, one launch (start us, length us, event | category | flops | bytes accessed | tf_op | source)
XLA Modules:
  0.0 140.2 jit_solution(15465903166070509834)
XLA Ops:
  0.6 136.6 %attn.1 = (bf16[2,7,384,128]{3,2,1,0:T(8,128)(2,1)}, bf16[2,7,384,128]{3,2,1,0:T(8,128)(2,1)}, bf16[2,384,128]{2,1,0:T(8,128)(2,1)}, bf16[2,384,128]{2,1,0:T(8,128)(2,1)}) custom-call(bf16[2,7,384,128]{3,2,1,0:T(8,128)(2,1)} %bitcast.12, bf16[2,7,384,128]{3,2,1,0:T(8,128)(2,1)} %bitcast.13, bf16[2,384,128]{2,1,0:T(8,128)(2,1)} %bitcast.14, ...), custom_call_target="tpu_custom_call" | custom-call | tf_op jit(solution)/shard_map/attn/pallas_call | solution.py:615
  137.3 2.9 %hand_over.1 = (bf16[2,7,384,128]{3,2,1,0:T(8,128)(2,1)}, bf16[2,7,384,128]{3,2,1,0:T(8,128)(2,1)}, bf16[2,384,128]{2,1,0:T(8,128)(2,1)}, bf16[2,384,128]{2,1,0:T(8,128)(2,1)}) custom-call(bf16[2,7,384,128]{3,2,1,0:T(8,128)(2,1)} %get-tuple-element.12.refs_0_, bf16[2,7,384,128]{3,2,1,0:T(8,128)(2,1)} %get-tuple-element.13.refs_1_, ...), custom_call_target="tpu_custom_call" | custom-call | tf_op jit(solution)/shard_map/hand_over/pallas_call | solution.py:637

commit v8 on v7

--- a/solution.py
+++ b/solution.py
@@ -104,7 +104,7 @@
         swap, local = kv_swap(i)
         local.wait()
         swap.wait_recv()
-    for h in (0, 1):
+    for h in (0, 1, 2):
         q_swap(h).start()
 
     def kv_up(p):
@@ -171,9 +171,9 @@
         def _():
             q_swap(jnp.minimum(h, heads - 1)).wait_recv()
 
-            @pl.when(h + 2 < n_own)
-            def _():
-                q_swap(jnp.minimum(h + 2, heads - 1)).start()
+            @pl.when(h + 3 < n_own)
+            def _():
+                q_swap(jnp.minimum(h + 3, heads - 1)).start()
 
             @pl.when(h + 2 == n_own)
             def _():

time: 140 us -> 140 us (level)
  no operation moved by 1% of the time
where the time goes in v8:
time: 140 us
  Pallas kernels  140 us (100%)
    pallas_call x1, Pallas kernels, local(): pl.pallas_call(functools.partial(kernel, heads), out_shape=[S(q.shape, BF...  137 us
    pallas_call x1, Pallas kernels, local(): pl.pallas_call(hand_over, out_shape=[S(t.shape, BF) for t in (o, dq, dk,...  2.88 us

profile of v8, /device:TPU:26, one launch (start us, length us, event | category | flops | bytes accessed | tf_op | source)
XLA Modules:
  0.0 140.2 jit_solution(1747300666669785425)
XLA Ops:
  0.6 136.6 %attn.1 = (bf16[2,7,384,128]{3,2,1,0:T(8,128)(2,1)}, bf16[2,7,384,128]{3,2,1,0:T(8,128)(2,1)}, bf16[2,384,128]{2,1,0:T(8,128)(2,1)}, bf16[2,384,128]{2,1,0:T(8,128)(2,1)}) custom-call(bf16[2,7,384,128]{3,2,1,0:T(8,128)(2,1)} %bitcast.12, bf16[2,7,384,128]{3,2,1,0:T(8,128)(2,1)} %bitcast.13, bf16[2,384,128]{2,1,0:T(8,128)(2,1)} %bitcast.14, ...), custom_call_target="tpu_custom_call" | custom-call | tf_op jit(solution)/shard_map/attn/pallas_call | solution.py:615
  137.3 2.9 %hand_over.1 = (bf16[2,7,384,128]{3,2,1,0:T(8,128)(2,1)}, bf16[2,7,384,128]{3,2,1,0:T(8,128)(2,1)}, bf16[2,384,128]{2,1,0:T(8,128)(2,1)}, bf16[2,384,128]{2,1,0:T(8,128)(2,1)}) custom-call(bf16[2,7,384,128]{3,2,1,0:T(8,128)(2,1)} %get-tuple-element.12.refs_0_, bf16[2,7,384,128]{3,2,1,0:T(8,128)(2,1)} %get-tuple-element.13.refs_1_, ...), custom_call_target="tpu_custom_call" | custom-call | tf_op jit(solution)/shard_map/hand_over/pallas_call | solution.py:637
